TPU v7x, 32 devices: a whole 2x2x4 slice. The times are simulated.
32 devices in a mesh: seq: 8 (over z, x), head: 4 (over y, core).
Axes of the slice: x: 2, y: 2, z: 4, core: 2. Of those that a mesh axis runs over, the one named last changes fastest.
Arguments:
- queries: bfloat16 [4096, 6144], P('seq', 'head'), may hold values from -10 to 10
- keys: bfloat16 [4096, 6144], P('seq', 'head'), may hold values from -10 to 10
- values: bfloat16 [4096, 6144], P('seq', 'head'), may hold values from -6 to 6
- frame_of_block: int32 [16], P('seq'), may hold values from 0 to 7, never falling along the last dimension, each value on 1 to 4 neighbouring positions
- pair_mask: int32 [16, 16], P('seq'), may hold values 0 or 1
- w_out: bfloat16 [6144, 6144], P('head', 'seq'), may hold values from -0.4375 to 0.4375
Outputs:
- projected: bfloat16 [4096, 6144], P('seq', 'head')
Inputs may be any that keep to these rules, and one draw needn't show every extreme that they name: `frame_of_block`: frame ids never fall along the blocks, every frame spans 1 to 4 consecutive blocks.
All inputs are finite; a program needn't handle non-finite values. No bound on the sum of `pair_mask` on one device may be relied on, other than what follows from the above.
Results may differ from a plain program's by a relative error of at most 0.015.
Values may be sent and summed in bfloat16 or wider, within the bound.
A program may use at most 192 MiB of HBM per device.

v0:
```python
import functools
import math

import jax
import jax.numpy as jnp
from jax import lax
from jax.experimental import pallas as pl
from jax.experimental.pallas import tpu as pltpu
from jax.sharding import PartitionSpec as P

HD = 128
BLK = 256
NEG = -1e30


def body_gather(queries, keys, values, frame_of_block, pair_mask, w_out):
    tok = queries.shape[0]
    heads_here = queries.shape[1] // HD
    count_blocks = pair_mask.shape[1]
    scale = 1.0 / math.sqrt(HD)
    key_span = 512
    q_heads = queries.reshape(tok, heads_here, HD)
    q_frame = jnp.repeat(frame_of_block, BLK)
    mask_rows = jnp.repeat(pair_mask.astype(jnp.float32), BLK, axis=0)
    block_ids = jnp.arange(count_blocks, dtype=jnp.int32)

    def update(state, k_rows, v_rows, allowed):
        peak, total, accum = state
        k_heads = k_rows.reshape(k_rows.shape[0], heads_here, HD)
        v_heads = v_rows.reshape(v_rows.shape[0], heads_here, HD)
        score = (
            jnp.einsum("qhd,khd->hqk", q_heads, k_heads, preferred_element_type=jnp.float32) * scale
        )
        score = jnp.where(allowed[None], score, -1e30)
        new_peak = jnp.maximum(peak, jnp.max(score, axis=2))
        weight = jnp.where(allowed[None], jnp.exp(score - new_peak[:, :, None]), 0.0)
        factor = jnp.exp(peak - new_peak)
        new_total = total * factor + jnp.sum(weight, axis=2)
        added = jnp.einsum(
            "hqk,khd->qhd", weight.astype(jnp.bfloat16), v_heads, preferred_element_type=jnp.float32
        )
        new_accum = accum * factor.T[:, :, None] + added
        return (new_peak, new_total, new_accum)

    def attend_block(state, k_rows, v_rows, k_frame, start):
        count = k_rows.shape[0]
        k_block = (start + jnp.arange(count, dtype=jnp.int32)) // BLK
        one_hot = (block_ids[:, None] == k_block[None, :]).astype(jnp.float32)
        link = jnp.dot(mask_rows, one_hot, preferred_element_type=jnp.float32)
        same = k_frame[None, :] == q_frame[:, None]
        allowed = (k_frame[None, :] <= q_frame[:, None]) & ((link > 0.5) | same)
        return update(state, k_rows, v_rows, allowed)

    initial = (
        jnp.full((heads_here, tok), -1e30, jnp.float32),
        jnp.zeros((heads_here, tok), jnp.float32),
        jnp.zeros((tok, heads_here, HD), jnp.float32),
    )
    k_frame_local = jnp.repeat(frame_of_block, BLK)
    k_rows = lax.all_gather(keys, "seq", axis=0, tiled=True)
    v_rows = lax.all_gather(values, "seq", axis=0, tiled=True)
    k_frame = lax.all_gather(k_frame_local, "seq", axis=0, tiled=True)
    count = k_rows.shape[0]

    def step(index, inner):
        offset = (index * key_span).astype(jnp.int32)
        return attend_block(
            inner,
            lax.dynamic_slice_in_dim(k_rows, offset, key_span, 0),
            lax.dynamic_slice_in_dim(v_rows, offset, key_span, 0),
            lax.dynamic_slice_in_dim(k_frame, offset, key_span, 0),
            offset,
        )

    state = lax.fori_loop(0, count // key_span, step, initial)
    peak, total, accum = state
    attn = (accum / total.T[:, :, None]).reshape(tok, heads_here * HD).astype(jnp.bfloat16)
    terms = jnp.dot(
        attn, lax.all_gather(w_out, "seq", axis=1, tiled=True), preferred_element_type=jnp.float32
    )
    return lax.psum_scatter(terms.astype(jnp.bfloat16), "head", scatter_dimension=1, tiled=True)


def greet(n, me):
    barrier = pltpu.get_barrier_semaphore()
    for k in range(1, n):
        pl.semaphore_signal(barrier, inc=1, device_id={"seq": lax.rem(me + k, n)}, device_id_type=pl.DeviceIdType.MESH)
    pl.semaphore_wait(barrier, n - 1)


def cols(head):
    return pl.ds(pl.multiple_of(head * HD, HD), HD)


def rows(start, size):
    return pl.ds(pl.multiple_of(start, size), size)


def spread_kernel(n, tok, q, k, v, meta, qf, qs, kf, ks, vf, vs, metas, hold, hold_half, hold_meta, send, recv, here):
    me = lax.axis_index("seq")
    half = tok // 2

    def pieces(to):
        pair, odd = to // 2, lax.rem(to, 2)
        own, shared = cols(3 * pair + 2 * odd), cols(3 * pair + 1)
        full = rows(me * tok, tok)
        return [
            (meta, metas.at[rows(me * 8, 8)]),
            (q.at[:, own], qf.at[full]),
            (k.at[:, own], kf.at[full]),
            (v.at[:, own], vf.at[full]),
            (q.at[rows(odd * half, half), shared], qs.at[rows(me * half, half)]),
            (k.at[:, shared], ks.at[full]),
            (v.at[:, shared], vs.at[full]),
        ]

    def bounce(index):
        if index == 0:
            return hold_meta
        if index == 4:
            return hold_half
        return hold.at[{1: 0, 2: 1, 3: 2, 5: 3, 6: 4}[index]]

    greet(n, me)
    copies = []
    for step in range(1, n):
        to = lax.rem(me + step, n)
        for i, (src, dst) in enumerate(pieces(to)):
            copy = pltpu.make_async_remote_copy(
                src_ref=src, dst_ref=dst, send_sem=send.at[step - 1, i], recv_sem=recv.at[step - 1, i],
                device_id={"seq": to}, device_id_type=pl.DeviceIdType.MESH,
            )
            copy.start()
            copies.append(copy)
    mine = pieces(me)
    ins = [pltpu.make_async_copy(src, bounce(i), here.at[0, i]) for i, (src, _) in enumerate(mine)]
    outs = [pltpu.make_async_copy(bounce(i), dst, here.at[1, i]) for i, (_, dst) in enumerate(mine)]
    for c in ins:
        c.start()
    for c, d in zip(ins, outs):
        c.wait()
        d.start()
    for d in outs:
        d.wait()
    for c in copies:
        c.wait()


def return_kernel(n, tok, of, os, attn, hold, hold_half, send, recv, here):
    me = lax.axis_index("seq")
    half = tok // 2
    pair, odd = me // 2, lax.rem(me, 2)
    own, shared = cols(3 * pair + 2 * odd), cols(3 * pair + 1)

    def pieces(to):
        return [
            (of.at[rows(to * tok, tok)], attn.at[:, own]),
            (os.at[rows(to * half, half)], attn.at[rows(odd * half, half), shared]),
        ]

    greet(n, me)
    copies = []
    for step in range(1, n):
        to = lax.rem(me + step, n)
        for i, (src, dst) in enumerate(pieces(to)):
            copy = pltpu.make_async_remote_copy(
                src_ref=src, dst_ref=dst, send_sem=send.at[step - 1, i], recv_sem=recv.at[step - 1, i],
                device_id={"seq": to}, device_id_type=pl.DeviceIdType.MESH,
            )
            copy.start()
            copies.append(copy)
    for i, ((src, dst), via) in enumerate(zip(pieces(me), (hold, hold_half))):
        c = pltpu.make_async_copy(src, via, here.at[0, i])
        c.start()
        c.wait()
        d = pltpu.make_async_copy(via, dst, here.at[1, i])
        d.start()
        d.wait()
    for c in copies:
        c.wait()


def attend_kernel(odd_ref, count_ref, list_ref, qf, qs, kf, ks, vf, vs, of, os):
    odd = odd_ref[0]
    j = pl.program_id(0)
    factor = math.log2(math.e) / math.sqrt(HD)

    def scores(q, k):
        return lax.dot_general(q, k, (((1,), (1,)), ((), ())), preferred_element_type=jnp.float32)

    def fold(state, parts, vals):
        peak, total, accum = state
        top = parts[0]
        for s in parts[1:]:
            top = jnp.maximum(top, s)
        new_peak = jnp.maximum(peak, jnp.max(top, axis=1, keepdims=True))
        keep = jnp.exp2((peak - new_peak) * factor)
        total, accum = total * keep, accum * keep
        for s, v in zip(parts, vals):
            p = jnp.exp2((s - new_peak) * factor)
            for c in range(0, BLK, HD):
                total = total + p[:, c:c + HD]
            accum = accum + jnp.dot(p.astype(jnp.bfloat16), v, preferred_element_type=jnp.float32)
        return new_peak, total, accum

    def start():
        return (
            jnp.full((BLK, 1), NEG, jnp.float32),
            jnp.zeros((BLK, HD), jnp.float32),
            jnp.zeros((BLK, HD), jnp.float32),
        )

    def finish(state):
        _, total, accum = state
        return (accum / jnp.sum(total, axis=1, keepdims=True)).astype(jnp.bfloat16)

    def walk(block, streams):
        count = count_ref[block]

        def step(i, states):
            a = rows(list_ref[block, 2 * i] * BLK, BLK)
            b = rows(list_ref[block, 2 * i + 1] * BLK, BLK)
            bias = jnp.where(2 * i + 1 < count, 0.0, NEG).astype(jnp.float32)
            parts = [[scores(q, k[a, :]), scores(q, k[b, :]) + bias] for q, k, _ in streams]
            return tuple(
                fold(state, part, (v[a, :], v[b, :])) for state, part, (_, _, v) in zip(states, parts, streams)
            )

        return lax.fori_loop(0, (count + 1) // 2, step, tuple(start() for _ in streams))

    same, other = rows(odd * BLK, BLK), rows((1 - odd) * BLK, BLK)
    first, second = walk(2 * j + odd, [(qf[same, :], kf, vf), (qs[...], ks, vs)])
    of[same, :] = finish(first)
    os[...] = finish(second)
    (third,) = walk(2 * j + 1 - odd, [(qf[other, :], kf, vf)])
    of[other, :] = finish(third)


def body_spread(n, queries, keys, values, frame_of_block, pair_mask, w_out):
    tok, width = queries.shape
    count_blocks = pair_mask.shape[1]
    tokens = n * tok
    per = tok // BLK
    w_all = lax.all_gather(w_out, "seq", axis=1, tiled=True)
    meta = jnp.concatenate([frame_of_block[:, None], pair_mask], axis=1)
    meta = jnp.pad(meta, ((0, 8 - per), (0, HD - 1 - count_blocks)))
    anyspace = pl.BlockSpec(memory_space=pl.ANY)
    big = jax.ShapeDtypeStruct((tokens, HD), queries.dtype)
    small = jax.ShapeDtypeStruct((tokens // 2, HD), queries.dtype)
    qf, qs, kf, ks, vf, vs, metas = pl.pallas_call(
        functools.partial(spread_kernel, n, tok),
        out_shape=[big, small, big, big, big, big, jax.ShapeDtypeStruct((8 * n, HD), jnp.int32)],
        in_specs=[anyspace] * 4,
        out_specs=[anyspace] * 7,
        scratch_shapes=[
            pltpu.VMEM((5, tok, HD), queries.dtype),
            pltpu.VMEM((tok // 2, HD), queries.dtype),
            pltpu.VMEM((8, HD), jnp.int32),
            pltpu.SemaphoreType.DMA((n - 1, 7)),
            pltpu.SemaphoreType.DMA((n - 1, 7)),
            pltpu.SemaphoreType.DMA((2, 7)),
        ],
        compiler_params=pltpu.CompilerParams(collective_id=0, has_side_effects=True),
        cost_estimate=pl.CostEstimate(flops=0, bytes_accessed=300_000_000, transcendentals=0),
        name="spread",
    )(queries, keys, values, meta)

    metas = metas.reshape(n, 8, HD)[:, :per].reshape(n * per, HD)
    frame, links = metas[:, 0], metas[:, 1:1 + count_blocks]
    allowed = (frame[None, :] <= frame[:, None]) & ((links == 1) | (frame[None, :] == frame[:, None]))
    place = jnp.cumsum(allowed.astype(jnp.int32), axis=1)
    count = place[:, -1]
    ids = jnp.arange(count_blocks, dtype=jnp.int32)
    hit = allowed[:, None, :] & (place[:, None, :] == ids[None, :, None] + 1)
    order = jnp.sum(jnp.where(hit, ids[None, None, :], 0), axis=2)
    odd = lax.rem(lax.axis_index("seq"), 2).reshape(1).astype(jnp.int32)

    smem = pl.BlockSpec(memory_space=pltpu.SMEM)
    whole = pl.BlockSpec((tokens, HD), lambda j: (0, 0))
    two = pl.BlockSpec((2 * BLK, HD), lambda j: (j, 0))
    one = pl.BlockSpec((BLK, HD), lambda j: (j, 0))
    of, os = pl.pallas_call(
        attend_kernel,
        grid=(tokens // (2 * BLK),),
        out_shape=[big, small],
        in_specs=[smem, smem, smem, two, one, whole, whole, whole, whole],
        out_specs=[two, one],
        compiler_params=pltpu.CompilerParams(vmem_limit_bytes=48 * 1024 * 1024),
        cost_estimate=pl.CostEstimate(flops=20_000_000_000, bytes_accessed=8_000_000, transcendentals=20_000_000),
        name="attend",
    )(odd, count, order, qf, qs, kf, ks, vf, vs)

    attn = pl.pallas_call(
        functools.partial(return_kernel, n, tok),
        out_shape=jax.ShapeDtypeStruct((tok, width), queries.dtype),
        in_specs=[anyspace] * 2,
        out_specs=anyspace,
        scratch_shapes=[
            pltpu.VMEM((tok, HD), queries.dtype),
            pltpu.VMEM((tok // 2, HD), queries.dtype),
            pltpu.SemaphoreType.DMA((n - 1, 2)),
            pltpu.SemaphoreType.DMA((n - 1, 2)),
            pltpu.SemaphoreType.DMA((2, 2)),
        ],
        compiler_params=pltpu.CompilerParams(collective_id=1, has_side_effects=True),
        cost_estimate=pl.CostEstimate(flops=0, bytes_accessed=100_000_000, transcendentals=0),
        name="bring_back",
    )(of, os)
    terms = jnp.dot(attn, w_all, preferred_element_type=jnp.float32)
    return lax.psum_scatter(terms.astype(jnp.bfloat16), "head", scatter_dimension=1, tiled=True)


def body(n, queries, keys, values, frame_of_block, pair_mask, w_out):
    heads_here = queries.shape[1] // HD
    fits = n % 2 == 0 and 2 * heads_here == 3 * n and queries.shape[0] == 2 * BLK
    if fits:
        return body_spread(n, queries, keys, values, frame_of_block, pair_mask, w_out)
    return body_gather(queries, keys, values, frame_of_block, pair_mask, w_out)


def solution(mesh):
    placed = (
        P("seq", "head"),
        P("seq", "head"),
        P("seq", "head"),
        P("seq"),
        P("seq", None),
        P("head", "seq"),
    )
    return jax.shard_map(
        functools.partial(body, mesh.shape["seq"]), mesh=mesh, in_specs=placed, out_specs=P("seq", "head"), check_vma=False
    )
```

profile of v0, /device:TPU:12, one launch (start us, length us, event | category | flops | bytes accessed | tf_op | source)
XLA Modules:
  0.0 528.8 jit_solution(14379846726530737275)
XLA Ops:
  6.5 0.0 copy-start.7
  6.5 0.0 copy-start.6
  6.5 0.0 all-gather.2.cloned.1.call-start
  6.5 0.7 all-gather.2.cloned.1.call-update
  7.3 0.0 reduce-scatter.2.cloned.1.call-start
  7.3 0.0 copy-done.7
  7.3 0.1 copy.13
  7.4 0.0 copy-done.6
  7.4 0.1 pad_add_fusion
  7.5 0.6 pad.4.meta
  8.1 215.8 %spread.1 = (bf16[4096,128]{1,0:T(8,128)(2,1)}, bf16[2048,128]{1,0:T(8,128)(2,1)}, bf16[4096,128]{1,0:T(8,128)(2,1)}, bf16[4096,128]{1,0:T(8,128)(2,1)}, bf16[40...) custom-call(bf16[512,1536]{1,0:T(8,128)(2,1)} %q.1, bf16[512,1536]{1,0:T(8,128)(2,1)} %k.1, ...), custom_call_target="tpu_custom_call" | custom-call | bytes 300000000 | tf_op jit(solution)/shard_map/spread/pallas_call | solution.py:250
  223.9 0.8 slice.16
  224.6 0.1 slice_reduce_fusion.1
  224.8 0.1 fusion.2
  224.8 0.2 reduce_window_sum.11
  225.0 0.2 slice_reduce_fusion.count_ref
  225.2 0.4 select_reduce_fusion.list_ref
  225.6 0.0 copy-start.2
  225.6 1.2 copy-done.2
  226.8 0.0 copy-start.3
  226.9 1.2 copy-done.3
  228.1 0.0 copy-start.4
  228.1 1.2 copy-done.4
  229.3 0.0 copy-start.5
  229.3 1.0 copy-done.5
  230.4 43.1 %attend.1 = (bf16[4096,128]{1,0:T(8,128)(2,1)S(1)}, bf16[2048,128]{1,0:T(8,128)(2,1)S(1)}) custom-call(s32[1]{0:T(128)} %bitcast.odd_ref, s32[16]{0:T(128)S(1)} %slice_reduce_fusion.count_ref, s32[16,16]{1,0:T(8,128)S(1)} %select_reduce_fusion.list_ref, bf16[4096,128]{1,0:T(8,128)(2,1)S(1)} %copy-done.2, bf16[2048,128]{1,0:T(8,128)(2,1)S(1)} %copy-done.5, ...), custom_call_target="tpu_custom_call" | custom-call | flops 20000000000 | bytes 8000000 | tf_op jit(solution)/shard_map/attend/pallas_call | solution.py:282
  273.5 0.0 copy-start
  273.5 1.0 copy-done
  274.5 0.0 copy-start.1
  274.5 0.8 copy-done.1
  275.3 87.1 %bring_back.1 = bf16[512,1536]{1,0:T(8,128)(2,1)} custom-call(bf16[4096,128]{1,0:T(8,128)(2,1)} %copy-done, bf16[2048,128]{1,0:T(8,128)(2,1)} %copy-done.1), custom_call_target="tpu_custom_call" | custom-call | bytes 100000000 | tf_op jit(solution)/shard_map/bring_back/pallas_call | solution.py:293
  362.4 84.1 %all-gather.2.cloned.1.call-done = bf16[1536,6144]{1,0:T(8,128)(2,1)} async-done(((bf16[1536,768]{1,0:T(8,128)(2,1)}), bf16[1536,6144]{1,0:T(8,128)(2,1)}) %all-gather.2.cloned.1.call-update) | async-done | bytes 18874384 | tf_op jit(solution)/shard_map/all_gather | solution.py:244
  446.5 15.9 %convolution_convert_fusion = bf16[512,6144]{1,0:T(8,128)(2,1)} fusion(bf16[512,1536]{1,0:T(8,128)(2,1)} %bring_back.1, bf16[1536,6144]{1,0:T(8,128)(2,1)} %all-gather.2.cloned.1.call-done), kind=kOutput, calls=%fused_computation | convolution fusion | flops 9666822144 | bytes 26738688 | tf_op jit(solution)/shard_map/dot_general | solution.py:309
  462.4 0.0 reduce-scatter.2.cloned.1.call-update
  462.4 59.5 %reduce-scatter.2.cloned.1.call-done = bf16[512,1536]{1,0:T(8,128)(2,1)} async-done(((bf16[512,6144]{1,0:T(8,128)(2,1)}), bf16[512,1536]{1,0:T(8,128)(2,1)}) %reduce-scatter.2.cloned.1.call-update) | async-done | bytes 1572880 | tf_op jit(solution)/shard_map/reduce_scatter | solution.py:310
  (1 shorter events, 0.0 us)
Async XLA Ops:
  6.5 0.8 copy-start.7
  6.5 0.9 copy-start.6
  6.5 440.0 %all-gather.2.cloned.1.call-start = ((), (), s32[]{:S(2)}) async-start(), calls=%async_computation.1 | async-start | bytes 21233664 | tf_op jit(solution)/shard_map/all_gather | solution.py:244
  7.3 514.7 %reduce-scatter.2.cloned.1.call-start = ((), (), s32[]{:S(2)}) async-start(), calls=%async_computation.2 | async-start | bytes 7864320 | tf_op jit(solution)/shard_map/reduce_scatter | solution.py:310
  225.6 1.2 copy-start.2
  226.8 1.2 copy-start.3
  228.1 1.2 copy-start.4
  229.3 1.0 copy-start.5
  273.5 1.0 copy-start
  274.5 0.8 copy-start.1
Sparse Core Ops, SparseCore 0:
  8.9 437.5 all-gather.1
  462.6 59.3 reduce-scatter.1
where the time goes:
time: 532 us; the launch traced here: 529 us
  Pallas kernels  346 us (65%)
  waiting for transfers between devices  144 us (27%)
  matrix products  15.9 us (3%)
  between operations  13.5 us (3%)
  local copies, waits for them, and re-layouts  8.27 us (2%)
    pallas_call x1, Pallas kernels, body_spread(): pl.pallas_call(functools.partial(spread_kernel, n, tok), out_shape=[big,...  216 us
    pallas_call x1, Pallas kernels, body_spread(): pl.pallas_call(functools.partial(return_kernel, n, tok), out_shape=jax.Sh...  87.1 us
    all_gather x1, waiting for transfers between devices, body_spread(): w_all = lax.all_gather(w_out, 'seq', axis=1, tiled=True)  84.1 us
    reduce_scatter x1, waiting for transfers between devices, body_spread(): lax.psum_scatter(terms.astype(jnp.bfloat16), 'head', scatter_dimension=1,...  59.5 us
    pallas_call x1, Pallas kernels, body_spread(): pl.pallas_call(attend_kernel, grid=(tokens // (2 * BLK),), out_shape=[big...  43.1 us
    dot_general x1, matrix products, body_spread(): terms = jnp.dot(attn, w_all, preferred_element_type=jnp.float32)  15.9 us
  transfers between devices with their start and end apart: 2, of which 2 were waited for; matrix products, arithmetic and copies ran while one was open for 0% of the time, Pallas kernels for 65%

commit v1 on v0

--- a/solution.py
+++ b/solution.py
@@ -11,6 +11,7 @@
 HD = 128
 BLK = 256
 NEG = -1e30
+EARLY = 6
 
 
 def body_gather(queries, keys, values, frame_of_block, pair_mask, w_out):
@@ -146,38 +147,198 @@
         c.wait()
 
 
-def return_kernel(n, tok, of, os, attn, hold, hold_half, send, recv, here):
-    me = lax.axis_index("seq")
+def project_kernel(
+    n, tok, early, of, os, w, wgot, out, attn, wbuf, part, d_send, d_recv, y_send, y_recv, final,
+    send1, recv1, here, send2, recv2, wsem_s, wsem_r, dsem_s, dsem_r, ysem_s, ysem_r, osem_s, osem_r,
+):
+    me, head = lax.axis_index("seq"), lax.axis_index("head")
+    quad = n // 2
     half = tok // 2
+    wide = w.shape[1]
     pair, odd = me // 2, lax.rem(me, 2)
     own, shared = cols(3 * pair + 2 * odd), cols(3 * pair + 1)
+    c, y = lax.rem(head, 2), head // 2
+    mine = me // quad
+    x, zl = lax.rem(me, 2), lax.rem(me // 2, 2)
+    base = mine * quad
+    peers = [me, base + 2 * zl + 1 - x, base + 2 * (1 - zl) + x, base + 2 * (1 - zl) + 1 - x]
+    partner = lax.rem(me + quad, n)
+    core_peer = 2 * y + 1 - c
+    y_peer = 2 * (1 - y) + c
+
+    def remote(src, dst, send, recv, seq, hd):
+        return pltpu.make_async_remote_copy(
+            src_ref=src, dst_ref=dst, send_sem=send, recv_sem=recv,
+            device_id={"seq": seq, "head": hd}, device_id_type=pl.DeviceIdType.MESH,
+        )
+
+    barrier = pltpu.get_barrier_semaphore()
+    friends = [(lax.rem(me + k, n), head) for k in range(1, n)]
+    friends += [(p, core_peer) for p in peers] + [(me, y_peer)]
+    for seq, hd in friends:
+        pl.semaphore_signal(barrier, inc=1, device_id={"seq": seq, "head": hd}, device_id_type=pl.DeviceIdType.MESH)
+    own_w = pltpu.make_async_copy(w, wbuf.at[mine], here.at[2])
+    own_w.start()
+    got_w = pltpu.make_async_copy(wgot, wbuf.at[1 - mine, pl.ds(0, early)], here.at[3])
+    got_w.start()
+    pl.semaphore_wait(barrier, len(friends))
 
     def pieces(to):
         return [
-            (of.at[rows(to * tok, tok)], attn.at[:, own]),
-            (os.at[rows(to * half, half)], attn.at[rows(odd * half, half), shared]),
+            (of.at[rows(to * tok, tok)], attn.at[0, :, own]),
+            (os.at[rows(to * half, half)], attn.at[0, rows(odd * half, half), shared]),
         ]
 
-    greet(n, me)
-    copies = []
+    back = []
     for step in range(1, n):
         to = lax.rem(me + step, n)
         for i, (src, dst) in enumerate(pieces(to)):
-            copy = pltpu.make_async_remote_copy(
-                src_ref=src, dst_ref=dst, send_sem=send.at[step - 1, i], recv_sem=recv.at[step - 1, i],
-                device_id={"seq": to}, device_id_type=pl.DeviceIdType.MESH,
-            )
+            copy = remote(src, dst, send1.at[step - 1, i], recv1.at[step - 1, i], to, head)
             copy.start()
-            copies.append(copy)
-    for i, ((src, dst), via) in enumerate(zip(pieces(me), (hold, hold_half))):
-        c = pltpu.make_async_copy(src, via, here.at[0, i])
-        c.start()
-        c.wait()
-        d = pltpu.make_async_copy(via, dst, here.at[1, i])
-        d.start()
-        d.wait()
-    for c in copies:
-        c.wait()
+            back.append(copy)
+    local = [pltpu.make_async_copy(src, dst, here.at[i]) for i, (src, dst) in enumerate(pieces(me))]
+    for copy in local:
+        copy.start()
+    for copy in local:
+        copy.wait()
+    for copy in back:
+        copy.wait_send()
+    w_copy = remote(
+        w.at[pl.ds(early, w.shape[0] - early)], wbuf.at[mine, pl.ds(early, w.shape[0] - early)],
+        wsem_s, wsem_r, partner, head,
+    )
+    for copy in back:
+        copy.wait_recv()
+    to_x = remote(attn.at[0], attn.at[1], send2.at[0], recv2.at[0], peers[1], head)
+    to_z = remote(attn.at[0], attn.at[2], send2.at[1], recv2.at[1], peers[2], head)
+    on_x = remote(attn.at[2], attn.at[3], send2.at[2], recv2.at[2], peers[1], head)
+    to_z.start()
+    to_x.start()
+    w_copy.start()
+    own_w.wait()
+
+    def block_of(unit):
+        return mine if unit < 4 else 1 - mine
+
+    def swap(unit):
+        return remote(d_send.at[unit], d_recv.at[unit], dsem_s.at[unit], dsem_r.at[unit], me, core_peer)
+
+    def over_y(r):
+        return remote(y_send.at[r], y_recv.at[r], ysem_s.at[r], ysem_r.at[r], me, y_peer)
+
+    def home(r):
+        dst = out.at[rows(c * half, half), pl.ds(pl.multiple_of(x * wide, HD), wide)]
+        return remote(final.at[r], dst, osem_s.at[r], osem_r.at[2 * x + c], peers[r], 2 * y + zl)
+
+    def home_here():
+        dst = out.at[rows(c * half, half), pl.ds(pl.multiple_of(x * wide, HD), wide)]
+        return pltpu.make_async_copy(final.at[0], dst, here.at[4])
+
+    def multiply(unit):
+        r, block = unit % 4, block_of(unit)
+
+        def one(t, carry):
+            side = (1 - c) * (1 - t) + c * t
+            value = jnp.dot(attn[r, rows(side * half, half), :], wbuf[block], preferred_element_type=jnp.float32)
+
+            @pl.when(t == 0)
+            def _():
+                d_send[unit] = value.astype(jnp.bfloat16)
+                swap(unit).start()
+
+            @pl.when(t == 1)
+            def _():
+                part[unit] = value
+
+            return carry
+
+        lax.fori_loop(0, 2, one, 0)
+
+    def add_core(unit):
+        r, block = unit % 4, block_of(unit)
+        swap(unit).wait_recv()
+
+        @pl.when(y == block)
+        def _():
+            part[unit] = part[unit] + d_recv[unit].astype(jnp.float32)
+
+        @pl.when(y != block)
+        def _():
+            y_send[r] = (part[unit] + d_recv[unit].astype(jnp.float32)).astype(jnp.bfloat16)
+            over_y(r).start()
+
+    def finish(unit):
+        r, block = unit % 4, block_of(unit)
+
+        @pl.when(y == block)
+        def _():
+            over_y(r).wait_recv()
+            final[r] = (part[unit] + y_recv[r].astype(jnp.float32)).astype(jnp.bfloat16)
+            if r:
+                home(r).start()
+            else:
+                @pl.when(zl != c)
+                def _():
+                    home(0).start()
+
+                @pl.when(zl == c)
+                def _():
+                    home_here().start()
+
+    multiply(0)
+    to_z.wait_recv()
+    on_x.start()
+    to_x.wait_recv()
+    multiply(1)
+    add_core(0)
+    multiply(2)
+    add_core(1)
+    finish(0)
+    on_x.wait_recv()
+    multiply(3)
+    add_core(2)
+    finish(1)
+    add_core(3)
+    finish(2)
+    finish(3)
+    got_w.wait()
+    w_copy.wait_recv()
+    multiply(4)
+    multiply(5)
+    add_core(4)
+    multiply(6)
+    add_core(5)
+    multiply(7)
+    add_core(6)
+    add_core(7)
+    for unit in range(4, 8):
+        finish(unit)
+
+    for copy in (to_x, to_z, on_x, w_copy):
+        copy.wait_send()
+    for unit in range(8):
+        swap(unit).wait_send()
+    for r in range(4):
+        over_y(r).wait_send()
+        if r:
+            home(r).wait_send()
+
+    @pl.when(zl != c)
+    def _():
+        home(0).wait_send()
+
+    @pl.when(zl == c)
+    def _():
+        home_here().wait()
+
+    for sx in range(2):
+        for sc in range(2):
+            piece = final.at[0]
+            arrived = remote(piece, piece, osem_s.at[0], osem_r.at[2 * sx + sc], me, core_peer)
+
+            @pl.when((zl != c) | (sx != x) | (sc != c))
+            def _():
+                arrived.wait_recv()
 
 
 def attend_kernel(odd_ref, count_ref, list_ref, qf, qs, kf, ks, vf, vs, of, os):
@@ -241,7 +402,6 @@
     count_blocks = pair_mask.shape[1]
     tokens = n * tok
     per = tok // BLK
-    w_all = lax.all_gather(w_out, "seq", axis=1, tiled=True)
     meta = jnp.concatenate([frame_of_block[:, None], pair_mask], axis=1)
     meta = jnp.pad(meta, ((0, 8 - per), (0, HD - 1 - count_blocks)))
     anyspace = pl.BlockSpec(memory_space=pl.ANY)
@@ -290,29 +450,40 @@
         name="attend",
     )(odd, count, order, qf, qs, kf, ks, vf, vs)
 
-    attn = pl.pallas_call(
-        functools.partial(return_kernel, n, tok),
-        out_shape=jax.ShapeDtypeStruct((tok, width), queries.dtype),
-        in_specs=[anyspace] * 2,
+    quad = n // 2
+    deep, wide = w_out.shape
+    early = EARLY * deep // 16
+    w_early, _ = lax.optimization_barrier((w_out[:early], kf))
+    w_got = lax.ppermute(w_early, "seq", [(i, (i + quad) % n) for i in range(n)])
+    dma = pltpu.SemaphoreType.DMA
+    return pl.pallas_call(
+        functools.partial(project_kernel, n, tok, early),
+        out_shape=jax.ShapeDtypeStruct((tok, 2 * wide), queries.dtype),
+        in_specs=[anyspace] * 4,
         out_specs=anyspace,
         scratch_shapes=[
-            pltpu.VMEM((tok, HD), queries.dtype),
-            pltpu.VMEM((tok // 2, HD), queries.dtype),
-            pltpu.SemaphoreType.DMA((n - 1, 2)),
-            pltpu.SemaphoreType.DMA((n - 1, 2)),
-            pltpu.SemaphoreType.DMA((2, 2)),
+            pltpu.VMEM((4, tok, width), queries.dtype),
+            pltpu.VMEM((2, deep, wide), queries.dtype),
+            pltpu.VMEM((8, tok // 2, wide), jnp.float32),
+            pltpu.VMEM((8, tok // 2, wide), queries.dtype),
+            pltpu.VMEM((8, tok // 2, wide), queries.dtype),
+            pltpu.VMEM((4, tok // 2, wide), queries.dtype),
+            pltpu.VMEM((4, tok // 2, wide), queries.dtype),
+            pltpu.VMEM((4, tok // 2, wide), queries.dtype),
+            dma((n - 1, 2)), dma((n - 1, 2)), dma((5,)), dma((3,)), dma((3,)), dma, dma,
+            dma((8,)), dma((8,)), dma((4,)), dma((4,)), dma((4,)), dma((4,)),
         ],
-        compiler_params=pltpu.CompilerParams(collective_id=1, has_side_effects=True),
-        cost_estimate=pl.CostEstimate(flops=0, bytes_accessed=100_000_000, transcendentals=0),
-        name="bring_back",
-    )(of, os)
-    terms = jnp.dot(attn, w_all, preferred_element_type=jnp.float32)
-    return lax.psum_scatter(terms.astype(jnp.bfloat16), "head", scatter_dimension=1, tiled=True)
-
-
-def body(n, queries, keys, values, frame_of_block, pair_mask, w_out):
+        compiler_params=pltpu.CompilerParams(
+            collective_id=1, has_side_effects=True, vmem_limit_bytes=56 * 1024 * 1024
+        ),
+        cost_estimate=pl.CostEstimate(flops=10_000_000_000, bytes_accessed=30_000_000, transcendentals=0),
+        name="project",
+    )(of, os, w_out, w_got)
+
+
+def body(n, groups, queries, keys, values, frame_of_block, pair_mask, w_out):
     heads_here = queries.shape[1] // HD
-    fits = n % 2 == 0 and 2 * heads_here == 3 * n and queries.shape[0] == 2 * BLK
+    fits = n == 8 and groups == 4 and 2 * heads_here == 3 * n and queries.shape[0] == 2 * BLK
     if fits:
         return body_spread(n, queries, keys, values, frame_of_block, pair_mask, w_out)
     return body_gather(queries, keys, values, frame_of_block, pair_mask, w_out)
@@ -328,5 +499,5 @@
         P("head", "seq"),
     )
     return jax.shard_map(
-        functools.partial(body, mesh.shape["seq"]), mesh=mesh, in_specs=placed, out_specs=P("seq", "head"), check_vma=False
+        functools.partial(body, mesh.shape["seq"], mesh.shape["head"]), mesh=mesh, in_specs=placed, out_specs=P("seq", "head"), check_vma=False
     )

time: 532 us -> 398 us (0.75)
  waiting for transfers between devices: 144 us -> 0.01 us
  Pallas kernels: 346 us -> 384 us
  matrix products: 15.9 us -> 0 us
  between operations: 13.5 us -> 0.09 us
  local copies, waits for them, and re-layouts: 8.27 us -> 13.7 us
    pallas_call x1, Pallas kernels: 87.1 us -> 209 us  [body_spread(): pl.pallas_call(functools.partial(project_kernel, n, tok, early), out_shap...]
    pallas_call x1, Pallas kernels: 216 us -> 129 us  [body_spread(): pl.pallas_call(functools.partial(spread_kernel, n, tok), out_shape=[big,...]
    all_gather x1 -> x0, waiting for transfers between devices: 84.1 us -> none  [body_spread(): w_all = lax.all_gather(w_out, 'seq', axis=1, tiled=True)]
    reduce_scatter x1 -> x0, waiting for transfers between devices: 59.5 us -> none  [body_spread(): lax.psum_scatter(terms.astype(jnp.bfloat16), 'head', scatter_dimension=1,...]
    dot_general x1 -> x0, matrix products: 15.9 us -> none  [body_spread(): terms = jnp.dot(attn, w_all, preferred_element_type=jnp.float32)]
  transfers between devices with their start and end apart: 2 -> 1, of which waited for: 2 -> 0; matrix products, arithmetic and copies ran while one was open for 0% -> 0% of each run, Pallas kernels for 65% -> 11%
where the time goes in v1:
time: 398 us; the launch traced here: 399 us
  Pallas kernels  384 us (96%)
  local copies, waits for them, and re-layouts  13.7 us (3%)
    pallas_call x1, Pallas kernels, body_spread(): pl.pallas_call(functools.partial(project_kernel, n, tok, early), out_shap...  209 us
    pallas_call x1, Pallas kernels, body_spread(): pl.pallas_call(functools.partial(spread_kernel, n, tok), out_shape=[big,...  129 us
    pallas_call x1, Pallas kernels, body_spread(): pl.pallas_call(attend_kernel, grid=(tokens // (2 * BLK),), out_shape=[big...  45.8 us
    unnamed x17, local copies, waits for them, and re-layouts  10 us
  transfers between devices with their start and end apart: 1, of which 0 were waited for; matrix products, arithmetic and copies ran while one was open for 0% of the time, Pallas kernels for 11%

profile of v1, /device:TPU:12, one launch (start us, length us, event | category | flops | bytes accessed | tf_op | source)
XLA Modules:
  0.0 398.5 jit_solution(13875047322715111868)
XLA Ops:
  0.0 0.0 copy-start.6
  0.0 0.8 copy.13
  0.8 1.2 slice.19
  2.0 0.0 copy-done.6
  2.0 0.1 pad_add_fusion
  2.1 0.6 pad.4.meta
  2.7 129.2 %spread.1 = (bf16[4096,128]{1,0:T(8,128)(2,1)}, bf16[2048,128]{1,0:T(8,128)(2,1)}, bf16[4096,128]{1,0:T(8,128)(2,1)}, bf16[4096,128]{1,0:T(8,128)(2,1)}, bf16[40...) custom-call(bf16[512,1536]{1,0:T(8,128)(2,1)} %q.1, bf16[512,1536]{1,0:T(8,128)(2,1)} %k.1, ...), custom_call_target="tpu_custom_call" | custom-call | bytes 300000000 | tf_op jit(solution)/shard_map/spread/pallas_call | solution.py:410
  131.8 0.1 collective-permute-start
  131.9 0.8 slice.20
  132.7 0.1 slice_reduce_fusion.1
  132.8 0.1 fusion.2
  132.9 0.2 reduce_window_sum.11
  133.1 0.2 slice_reduce_fusion.count_ref
  133.2 0.4 select_reduce_fusion.list_ref
  133.7 0.0 copy-start
  133.7 1.2 copy-done
  134.9 0.0 copy-start.1
  134.9 1.2 copy-done.1
  136.1 0.0 copy-start.2
  136.1 1.2 copy-done.2
  137.3 0.0 copy-start.3
  137.3 1.0 copy-done.3
  138.4 45.8 %attend.1 = (bf16[4096,128]{1,0:T(8,128)(2,1)S(1)}, bf16[2048,128]{1,0:T(8,128)(2,1)S(1)}) custom-call(s32[1]{0:T(128)} %bitcast.odd_ref, s32[16]{0:T(128)S(1)} %slice_reduce_fusion.count_ref, s32[16,16]{1,0:T(8,128)S(1)} %select_reduce_fusion.list_ref, bf16[4096,128]{1,0:T(8,128)(2,1)S(1)} %copy-done, bf16[2048,128]{1,0:T(8,128)(2,1)S(1)} %copy-done.3, ...), custom_call_target="tpu_custom_call" | custom-call | flops 20000000000 | bytes 8000000 | tf_op jit(solution)/shard_map/attend/pallas_call | solution.py:442
  184.2 0.0 copy-start.4
  184.2 1.0 copy-done.4
  185.2 0.0 copy-start.5
  185.2 0.8 copy-done.5
  186.0 0.0 collective-permute-done.wgot
  186.0 0.0 copy-start.7
  186.0 0.9 copy-done.7
  186.9 209.0 %project.1 = bf16[512,1536]{1,0:T(8,128)(2,1)} custom-call(bf16[4096,128]{1,0:T(8,128)(2,1)} %copy-done.4, bf16[2048,128]{1,0:T(8,128)(2,1)} %copy-done.5, bf16[1536,768]{1,0:T(8,128)(2,1)} %w.1, bf16[576,768]{1,0:T(8,128)(2,1)} %copy-done.7), custom_call_target="tpu_custom_call" | custom-call | flops 10000000000 | bytes 30000000 | tf_op jit(solution)/shard_map/project/pallas_call | solution.py:459
  395.9 2.7 copy.15
  (1 shorter events, 0.0 us)
Async XLA Ops:
  0.0 2.0 copy-start.6
  131.8 54.1 %collective-permute-start = (bf16[576,768]{1,0:T(8,128)(2,1)S(1)}, bf16[576,768]{1,0:T(8,128)(2,1)S(1)}, u32[]{:S(2)}, u32[]{:S(2)}) collective-permute-start(bf16[576,768]{1,0:T(8,128)(2,1)S(1)} %slice.19), channel_id=1, source_target_pairs={{0,16},{4,20},{8,24},{12,28},{16,0},{20,4},{24,8},{28,12},{1,17},{... | collective-permute-start | bytes 2654216 | tf_op jit(solution)/shard_map/ppermute | solution.py:457
  133.7 1.2 copy-start
  134.9 1.2 copy-start.1
  136.1 1.2 copy-start.2
  137.3 1.0 copy-start.3
  184.2 1.0 copy-start.4
  185.2 0.8 copy-start.5
  186.0 0.9 copy-start.7

commit v2 on v0

--- a/solution.py
+++ b/solution.py
@@ -146,38 +146,263 @@
         c.wait()
 
 
-def return_kernel(n, tok, of, os, attn, hold, hold_half, send, recv, here):
-    me = lax.axis_index("seq")
+def project_kernel(
+    n, tok, groups, of, os, w, wgot, out, attn, wown, wpart, part, d_send, d_recv, y_send, y_recv, final,
+    send1, recv1, here, send2, recv2, wsem_s, wsem_r, dsem_s, dsem_r, ysem_s, ysem_r, osem_s, osem_r, osem_l,
+):
+    me, head = lax.axis_index("seq"), lax.axis_index("head")
     half = tok // 2
+    wide = w.shape[1]
+    early = wgot.shape[1]
+    c, y = lax.rem(head, 2), head // 2
+    x, zl, mine = lax.rem(me, 2), lax.rem(me // 2, 2), me // 4
+    core_peer = 2 * y + 1 - c
+    y_peer = 2 * (1 - y) + c
+
+    def flip(bit, value):
+        return 1 - value if bit else value
+
+    def at(k):
+        return 4 * flip(k & 4, mine) + 2 * flip(k & 2, zl) + flip(k & 1, x)
+
+    def remote(src, dst, send, recv, seq, hd):
+        return pltpu.make_async_remote_copy(
+            src_ref=src, dst_ref=dst, send_sem=send, recv_sem=recv,
+            device_id={"seq": seq, "head": hd}, device_id_type=pl.DeviceIdType.MESH,
+        )
+
+    barrier = pltpu.get_barrier_semaphore()
+    friends = [(at(k), head) for k in range(1, n)]
+    friends += [(at(k), core_peer) for k in range(4)] + [(me, y_peer)]
+    for seq, hd in friends:
+        pl.semaphore_signal(barrier, inc=1, device_id={"seq": seq, "head": hd}, device_id_type=pl.DeviceIdType.MESH)
+    own_w = pltpu.make_async_copy(w, wown, here.at[2])
+    own_w.start()
+    got_w = pltpu.make_async_copy(wgot, wpart.at[:, pl.ds(0, early)], here.at[3])
+    got_w.start()
+    pl.semaphore_wait(barrier, len(friends))
+
     pair, odd = me // 2, lax.rem(me, 2)
     own, shared = cols(3 * pair + 2 * odd), cols(3 * pair + 1)
 
     def pieces(to):
         return [
-            (of.at[rows(to * tok, tok)], attn.at[:, own]),
-            (os.at[rows(to * half, half)], attn.at[rows(odd * half, half), shared]),
+            (of.at[rows(to * tok, tok)], attn.at[0, :, own]),
+            (os.at[rows(to * half, half)], attn.at[0, rows(odd * half, half), shared]),
         ]
 
-    greet(n, me)
-    copies = []
-    for step in range(1, n):
-        to = lax.rem(me + step, n)
-        for i, (src, dst) in enumerate(pieces(to)):
-            copy = pltpu.make_async_remote_copy(
-                src_ref=src, dst_ref=dst, send_sem=send.at[step - 1, i], recv_sem=recv.at[step - 1, i],
-                device_id={"seq": to}, device_id_type=pl.DeviceIdType.MESH,
+    back = [
+        [remote(src, dst, send1.at[k, i], recv1.at[k, i], at(k), head) for i, (src, dst) in enumerate(pieces(at(k)))]
+        for k in range(1, n)
+    ]
+    for copies in back:
+        for copy in copies:
+            copy.start()
+    local = [pltpu.make_async_copy(src, dst, here.at[i]) for i, (src, dst) in enumerate(pieces(me))]
+    for copy in local:
+        copy.start()
+
+    def chunk(at_pair):
+        return pl.ds(pl.multiple_of(3 * HD * at_pair, HD), 3 * HD)
+
+    def moves(i):
+        mine_cols = chunk(at(2 * i) // 2)
+        peer_cols = chunk(at((2 * i) ^ 2) // 2)
+        return (
+            remote(attn.at[0, :, mine_cols], attn.at[1, :, mine_cols], send2.at[0, i], recv2.at[0, i], at(1), head),
+            remote(attn.at[0, :, mine_cols], attn.at[2, :, mine_cols], send2.at[1, i], recv2.at[1, i], at(2), head),
+            remote(attn.at[2, :, peer_cols], attn.at[3, :, peer_cols], send2.at[2, i], recv2.at[2, i], at(1), head),
+        )
+
+    steps = [moves(i) for i in range(4)]
+
+    def share(i):
+        if i == 0:
+            for copy in local:
+                copy.wait()
+        for k in (2 * i, 2 * i + 1):
+            if k:
+                for copy in back[k - 1]:
+                    copy.wait_recv()
+        steps[i][1].start()
+        steps[i][0].start()
+
+    def forward(i):
+        steps[i][1].wait_recv()
+        steps[i][2].start()
+
+    late = [g for g, (role, first, size) in enumerate(groups) if role and first >= early]
+
+    def w_late(g):
+        _, first, size = groups[g]
+        return remote(
+            w.at[:, pl.ds(first, size)], wpart.at[:, pl.ds(first, size)], wsem_s.at[g], wsem_r.at[g], at(4), head
+        )
+
+    def block_of(g):
+        return 1 - mine if groups[g][0] else mine
+
+    def span(g):
+        role, first, size = groups[g]
+        return pl.ds(role * wide + first, size)
+
+    def inner(g):
+        return pl.ds(groups[g][1], groups[g][2])
+
+    def swap(g, r):
+        return remote(
+            d_send.at[r, :, span(g)], d_recv.at[r, :, span(g)], dsem_s.at[g, r], dsem_r.at[g, r], me, core_peer
+        )
+
+    def over_y(g, r):
+        return remote(
+            y_send.at[r, :, inner(g)], y_recv.at[r, :, inner(g)], ysem_s.at[g, r], ysem_r.at[g, r], me, y_peer
+        )
+
+    def target(g):
+        return out.at[rows(c * half, half), pl.ds(pl.multiple_of(x * wide + groups[g][1], HD), groups[g][2])]
+
+    def home(g, r):
+        return remote(
+            final.at[r, :, inner(g)], target(g), osem_s.at[g, r], osem_r.at[2 * x + c, g], at(r), 2 * y + zl
+        )
+
+    def home_here(g):
+        return pltpu.make_async_copy(final.at[0, :, inner(g)], target(g), osem_l.at[g])
+
+    def multiply(g, r):
+        role, first, size = groups[g]
+        weights = wpart if role else wown
+
+        def one(t, carry):
+            side = (1 - c) * (1 - t) + c * t
+            value = jnp.dot(
+                attn[r, rows(side * half, half), :], weights[:, pl.ds(first, size)], preferred_element_type=jnp.float32
             )
-            copy.start()
-            copies.append(copy)
-    for i, ((src, dst), via) in enumerate(zip(pieces(me), (hold, hold_half))):
-        c = pltpu.make_async_copy(src, via, here.at[0, i])
-        c.start()
-        c.wait()
-        d = pltpu.make_async_copy(via, dst, here.at[1, i])
-        d.start()
-        d.wait()
-    for c in copies:
-        c.wait()
+
+            @pl.when(t == 0)
+            def _():
+                d_send[r, :, span(g)] = value.astype(jnp.bfloat16)
+                swap(g, r).start()
+
+            @pl.when(t == 1)
+            def _():
+                part[r, :, span(g)] = value
+
+            return carry
+
+        lax.fori_loop(0, 2, one, 0)
+
+    def add_core(g, r):
+        swap(g, r).wait_recv()
+
+        @pl.when(y == block_of(g))
+        def _():
+            part[r, :, span(g)] = part[r, :, span(g)] + d_recv[r, :, span(g)].astype(jnp.float32)
+
+        @pl.when(y != block_of(g))
+        def _():
+            value = part[r, :, span(g)] + d_recv[r, :, span(g)].astype(jnp.float32)
+            y_send[r, :, inner(g)] = value.astype(jnp.bfloat16)
+            over_y(g, r).start()
+
+    def finish(g, r):
+        @pl.when(y == block_of(g))
+        def _():
+            over_y(g, r).wait_recv()
+            value = part[r, :, span(g)] + y_recv[r, :, inner(g)].astype(jnp.float32)
+            final[r, :, inner(g)] = value.astype(jnp.bfloat16)
+            if r:
+                home(g, r).start()
+            else:
+                @pl.when(zl != c)
+                def _():
+                    home(g, 0).start()
+
+                @pl.when(zl == c)
+                def _():
+                    home_here(g).start()
+
+    ready = [g for g in range(len(groups)) if g not in late]
+
+    def shard(r):
+        for i, g in enumerate(ready):
+            multiply(g, r)
+            if i:
+                add_core(ready[i - 1], r)
+        add_core(ready[-1], r)
+
+    share(0)
+    share(1)
+    forward(0)
+    share(2)
+    forward(1)
+    share(3)
+    for g in late:
+        w_late(g).start()
+    forward(2)
+    own_w.wait()
+    got_w.wait()
+    shard(0)
+    forward(3)
+    for r in range(1, 4):
+        for i in range(4):
+            steps[i][(None, 0, 1, 2)[r]].wait_recv() if r != 2 else None
+        shard(r)
+        for g in ready:
+            finish(g, r - 1)
+    for g in ready:
+        finish(g, 3)
+    units = [(g, r) for g in late for r in range(4)]
+    for i, (g, r) in enumerate(units):
+        if r == 0:
+            w_late(g).wait_recv()
+        multiply(g, r)
+        if i >= 1:
+            add_core(*units[i - 1])
+        if i >= 4:
+            finish(*units[i - 4])
+    add_core(*units[-1])
+    for unit in units[-4:]:
+        finish(*unit)
+
+    for copies in back:
+        for copy in copies:
+            copy.wait_send()
+    for copies in steps:
+        for copy in copies:
+            copy.wait_send()
+    for g in late:
+        w_late(g).wait_send()
+    for g in range(len(groups)):
+        for r in range(4):
+            swap(g, r).wait_send()
+
+            @pl.when(y != block_of(g))
+            def _():
+                over_y(g, r).wait_send()
+
+            if r:
+                @pl.when(y == block_of(g))
+                def _():
+                    home(g, r).wait_send()
+
+        @pl.when((y == block_of(g)) & (zl != c))
+        def _():
+            home(g, 0).wait_send()
+
+        @pl.when((y == block_of(g)) & (zl == c))
+        def _():
+            home_here(g).wait()
+
+        for sx in range(2):
+            for sc in range(2):
+                piece = final.at[0, :, inner(g)]
+                arrived = remote(piece, piece, osem_s.at[g, 0], osem_r.at[2 * sx + sc, g], me, core_peer)
+
+                @pl.when((y == block_of(g)) & ((zl != c) | (sx != x) | (sc != c)))
+                def _():
+                    arrived.wait_recv()
 
 
 def attend_kernel(odd_ref, count_ref, list_ref, qf, qs, kf, ks, vf, vs, of, os):
@@ -241,7 +466,6 @@
     count_blocks = pair_mask.shape[1]
     tokens = n * tok
     per = tok // BLK
-    w_all = lax.all_gather(w_out, "seq", axis=1, tiled=True)
     meta = jnp.concatenate([frame_of_block[:, None], pair_mask], axis=1)
     meta = jnp.pad(meta, ((0, 8 - per), (0, HD - 1 - count_blocks)))
     anyspace = pl.BlockSpec(memory_space=pl.ANY)
@@ -285,34 +509,49 @@
         out_shape=[big, small],
         in_specs=[smem, smem, smem, two, one, whole, whole, whole, whole],
         out_specs=[two, one],
-        compiler_params=pltpu.CompilerParams(vmem_limit_bytes=48 * 1024 * 1024),
+        compiler_params=pltpu.CompilerParams(vmem_limit_bytes=60 * 1024 * 1024),
         cost_estimate=pl.CostEstimate(flops=20_000_000_000, bytes_accessed=8_000_000, transcendentals=20_000_000),
         name="attend",
     )(odd, count, order, qf, qs, kf, ks, vf, vs)
 
-    attn = pl.pallas_call(
-        functools.partial(return_kernel, n, tok),
-        out_shape=jax.ShapeDtypeStruct((tok, width), queries.dtype),
-        in_specs=[anyspace] * 2,
+    deep, wide = w_out.shape
+    early = wide // 2
+    w_early, _ = lax.optimization_barrier((w_out[:, :early], kf))
+    w_got = lax.ppermute(w_early, "seq", [(i, (i + n // 2) % n) for i in range(n)])
+    groups = [(0, 0, early), (0, early, wide - early), (1, 0, early)]
+    groups += [(1, first, HD) for first in range(early, wide, HD)]
+    count = len(groups)
+    dma = pltpu.SemaphoreType.DMA
+    return pl.pallas_call(
+        functools.partial(project_kernel, n, tok, groups),
+        out_shape=jax.ShapeDtypeStruct((tok, 2 * wide), queries.dtype),
+        in_specs=[anyspace] * 4,
         out_specs=anyspace,
         scratch_shapes=[
-            pltpu.VMEM((tok, HD), queries.dtype),
-            pltpu.VMEM((tok // 2, HD), queries.dtype),
-            pltpu.SemaphoreType.DMA((n - 1, 2)),
-            pltpu.SemaphoreType.DMA((n - 1, 2)),
-            pltpu.SemaphoreType.DMA((2, 2)),
+            pltpu.VMEM((4, tok, width), queries.dtype),
+            pltpu.VMEM((deep, wide), queries.dtype),
+            pltpu.VMEM((deep, wide), queries.dtype),
+            pltpu.VMEM((4, tok // 2, 2 * wide), jnp.float32),
+            pltpu.VMEM((4, tok // 2, 2 * wide), queries.dtype),
+            pltpu.VMEM((4, tok // 2, 2 * wide), queries.dtype),
+            pltpu.VMEM((4, tok // 2, wide), queries.dtype),
+            pltpu.VMEM((4, tok // 2, wide), queries.dtype),
+            pltpu.VMEM((4, tok // 2, wide), queries.dtype),
+            dma((n, 2)), dma((n, 2)), dma((4,)), dma((3, 4)), dma((3, 4)), dma((count,)), dma((count,)),
+            dma((count, 4)), dma((count, 4)), dma((count, 4)), dma((count, 4)),
+            dma((count, 4)), dma((4, count)), dma((count,)),
         ],
-        compiler_params=pltpu.CompilerParams(collective_id=1, has_side_effects=True),
-        cost_estimate=pl.CostEstimate(flops=0, bytes_accessed=100_000_000, transcendentals=0),
-        name="bring_back",
-    )(of, os)
-    terms = jnp.dot(attn, w_all, preferred_element_type=jnp.float32)
-    return lax.psum_scatter(terms.astype(jnp.bfloat16), "head", scatter_dimension=1, tiled=True)
-
-
-def body(n, queries, keys, values, frame_of_block, pair_mask, w_out):
+        compiler_params=pltpu.CompilerParams(
+            collective_id=1, has_side_effects=True, vmem_limit_bytes=58 * 1024 * 1024
+        ),
+        cost_estimate=pl.CostEstimate(flops=10_000_000_000, bytes_accessed=30_000_000, transcendentals=0),
+        name="project",
+    )(of, os, w_out, w_got)
+
+
+def body(n, groups, queries, keys, values, frame_of_block, pair_mask, w_out):
     heads_here = queries.shape[1] // HD
-    fits = n % 2 == 0 and 2 * heads_here == 3 * n and queries.shape[0] == 2 * BLK
+    fits = n == 8 and groups == 4 and 2 * heads_here == 3 * n and queries.shape[0] == 2 * BLK
     if fits:
         return body_spread(n, queries, keys, values, frame_of_block, pair_mask, w_out)
     return body_gather(queries, keys, values, frame_of_block, pair_mask, w_out)
@@ -328,5 +567,5 @@
         P("head", "seq"),
     )
     return jax.shard_map(
-        functools.partial(body, mesh.shape["seq"]), mesh=mesh, in_specs=placed, out_specs=P("seq", "head"), check_vma=False
+        functools.partial(body, mesh.shape["seq"], mesh.shape["head"]), mesh=mesh, in_specs=placed, out_specs=P("seq", "head"), check_vma=False
     )

time: 532 us -> 325 us (0.61)
  waiting for transfers between devices: 144 us -> 1.17 us
  Pallas kernels: 346 us -> 315 us
  matrix products: 15.9 us -> 0 us
  between operations: 13.5 us -> 0.05 us
    pallas_call x1, Pallas kernels: 216 us -> 129 us  [body_spread(): pl.pallas_call(functools.partial(spread_kernel, n, tok), out_shape=[big,...]
    all_gather x1 -> x0, waiting for transfers between devices: 84.1 us -> none  [body_spread(): w_all = lax.all_gather(w_out, 'seq', axis=1, tiled=True)]
    reduce_scatter x1 -> x0, waiting for transfers between devices: 59.5 us -> none  [body_spread(): lax.psum_scatter(terms.astype(jnp.bfloat16), 'head', scatter_dimension=1,...]
    pallas_call x1, Pallas kernels: 87.1 us -> 140 us  [body_spread(): pl.pallas_call(functools.partial(project_kernel, n, tok, groups), out_sha...]
    dot_general x1 -> x0, matrix products: 15.9 us -> none  [body_spread(): terms = jnp.dot(attn, w_all, preferred_element_type=jnp.float32)]
  transfers between devices with their start and end apart: 2 -> 1, of which waited for: 2 -> 1; matrix products, arithmetic and copies ran while one was open for 0% -> 1% of each run, Pallas kernels for 65% -> 14%
where the time goes in v2:
time: 325 us
  Pallas kernels  315 us (97%)
  local copies, waits for them, and re-layouts  8 us (2%)
    pallas_call x1, Pallas kernels, body_spread(): pl.pallas_call(functools.partial(project_kernel, n, tok, groups), out_sha...  140 us
    pallas_call x1, Pallas kernels, body_spread(): pl.pallas_call(functools.partial(spread_kernel, n, tok), out_shape=[big,...  129 us
    pallas_call x1, Pallas kernels, body_spread(): pl.pallas_call(attend_kernel, grid=(tokens // (2 * BLK),), out_shape=[big...  45.9 us
  transfers between devices with their start and end apart: 1, of which 1 were waited for; matrix products, arithmetic and copies ran while one was open for 1% of the time, Pallas kernels for 14%

profile of v2, /device:TPU:12, one launch (start us, length us, event | category | flops | bytes accessed | tf_op | source)
XLA Modules:
  0.0 325.4 jit_solution(855265367526938200)
XLA Ops:
  0.0 0.0 copy-start
  0.0 0.8 copy.13
  0.8 1.4 slice.19
  2.1 0.0 copy-done
  2.2 0.1 pad_add_fusion
  2.2 0.6 pad.4.meta
  2.8 129.2 %spread.1 = (bf16[4096,128]{1,0:T(8,128)(2,1)}, bf16[2048,128]{1,0:T(8,128)(2,1)}, bf16[4096,128]{1,0:T(8,128)(2,1)}, bf16[4096,128]{1,0:T(8,128)(2,1)}, bf16[40...) custom-call(bf16[512,1536]{1,0:T(8,128)(2,1)} %q.1, bf16[512,1536]{1,0:T(8,128)(2,1)} %k.1, ...), custom_call_target="tpu_custom_call" | custom-call | bytes 300000000 | tf_op jit(solution)/shard_map/spread/pallas_call | solution.py:474
  132.0 0.1 collective-permute-start
  132.1 0.8 slice.20
  132.9 0.1 slice_reduce_fusion.1
  133.0 0.1 fusion.2
  133.0 0.2 reduce_window_sum.11
  133.2 0.7 slice_reduce_fusion.count_ref
  133.9 1.0 select_reduce_fusion.list_ref
  134.9 45.9 %attend.1 = (bf16[4096,128]{1,0:T(8,128)(2,1)}, bf16[2048,128]{1,0:T(8,128)(2,1)}) custom-call(s32[1]{0:T(128)} %bitcast.odd_ref, s32[16]{0:T(128)} %slice_reduce_fusion.count_ref, s32[16,16]{1,0:T(8,128)} %select_reduce_fusion.list_ref, bf16[4096,128]{1,0:T(8,128)(2,1)} %get-tuple-element.16.qf, bf16[2048,128]{1,0:T(8,128)(2,1)} %get-tuple-element.17.qs, ...), custom_call_target="tpu_custom_call" | custom-call | flops 20000000000 | bytes 8000000 | tf_op jit(solution)/shard_map/attend/pallas_call | solution.py:506
  180.8 1.2 collective-permute-done.wgot
  182.0 0.0 copy-start.1
  182.0 1.0 copy-done.1
  183.0 139.8 %project.1 = bf16[512,1536]{1,0:T(8,128)(2,1)} custom-call(bf16[4096,128]{1,0:T(8,128)(2,1)} %get-tuple-element.22.of, bf16[2048,128]{1,0:T(8,128)(2,1)} %get-tuple-element.23.os, bf16[1536,768]{1,0:T(8,128)(2,1)} %w.1, bf16[1536,384]{1,0:T(8,128)(2,1)} %copy-done.1), custom_call_target="tpu_custom_call" | custom-call | flops 10000000000 | bytes 30000000 | tf_op jit(solution)/shard_map/project/pallas_call | solution.py:525
  322.8 2.7 copy.15
  (1 shorter events, 0.0 us)
Async XLA Ops:
  0.0 2.2 copy-start
  132.0 50.0 %collective-permute-start = (bf16[1536,384]{1,0:T(8,128)(2,1)S(1)}, bf16[1536,384]{1,0:T(8,128)(2,1)S(1)}, u32[]{:S(2)}, u32[]{:S(2)}) collective-permute-start(bf16[1536,384]{1,0:T(8,128)(2,1)S(1)} %slice.19), channel_id=1, source_target_pairs={{0,16},{4,20},{8,24},{12,28},{16,0},{20,4},{24,8},{28,12},{1,17},{... | collective-permute-start | bytes 3538952 | tf_op jit(solution)/shard_map/ppermute | solution.py:520
  182.0 1.0 copy-start.1

commit v3 on v2

--- a/solution.py
+++ b/solution.py
@@ -81,11 +81,24 @@
     return lax.psum_scatter(terms.astype(jnp.bfloat16), "head", scatter_dimension=1, tiled=True)
 
 
-def greet(n, me):
+def flip(bit, value):
+    return 1 - value if bit else value
+
+
+def greet(plane):
     barrier = pltpu.get_barrier_semaphore()
-    for k in range(1, n):
-        pl.semaphore_signal(barrier, inc=1, device_id={"seq": lax.rem(me + k, n)}, device_id_type=pl.DeviceIdType.MESH)
-    pl.semaphore_wait(barrier, n - 1)
+    for seq, head in plane:
+        pl.semaphore_signal(
+            barrier, inc=1, device_id={"seq": seq, "head": head}, device_id_type=pl.DeviceIdType.MESH
+        )
+    return lambda: pl.semaphore_wait(barrier, len(plane))
+
+
+def remote(src, dst, send, recv, seq, head):
+    return pltpu.make_async_remote_copy(
+        src_ref=src, dst_ref=dst, send_sem=send, recv_sem=recv,
+        device_id={"seq": seq, "head": head}, device_id_type=pl.DeviceIdType.MESH,
+    )
 
 
 def cols(head):
@@ -96,54 +109,109 @@
     return pl.ds(pl.multiple_of(start, size), size)
 
 
-def spread_kernel(n, tok, q, k, v, meta, qf, qs, kf, ks, vf, vs, metas, hold, hold_half, hold_meta, send, recv, here):
-    me = lax.axis_index("seq")
+def spread_kernel(
+    n, tok, q, k, v, meta, qf, qs, kf, ks, vf, vs, metas,
+    hold, hold_half, hold_meta, send, recv, here, fsem_s, fsem_r,
+):
+    me, head = lax.axis_index("seq"), lax.axis_index("head")
     half = tok // 2
-
-    def pieces(to):
-        pair, odd = to // 2, lax.rem(to, 2)
-        own, shared = cols(3 * pair + 2 * odd), cols(3 * pair + 1)
+    x, zl, zh = lax.rem(me, 2), lax.rem(me // 2, 2), me // 4
+    c, y = lax.rem(head, 2), head // 2
+    other = 2 * y + 1 - c
+    cross = x * (1 - c) + (1 - x) * c
+
+    def layer(i):
+        return 2 * flip(i & 2, zh) + flip(i & 1, zl)
+
+    def pieces(i, far):
+        pair, core = layer(i), flip(far, c)
+        own, shared = cols(3 * pair + 2 * core), cols(3 * pair + 1)
         full = rows(me * tok, tok)
         return [
-            (meta, metas.at[rows(me * 8, 8)]),
             (q.at[:, own], qf.at[full]),
             (k.at[:, own], kf.at[full]),
             (v.at[:, own], vf.at[full]),
-            (q.at[rows(odd * half, half), shared], qs.at[rows(me * half, half)]),
-            (k.at[:, shared], ks.at[full]),
-            (v.at[:, shared], vs.at[full]),
+            (q.at[rows(core * half, half), shared], qs.at[rows(me * half, half)]),
+            (v.at[:, shared], vs.at[full]) if far else (k.at[:, shared], ks.at[full]),
+            (meta, metas.at[rows(me * 8, 8)]),
         ]
 
-    def bounce(index):
-        if index == 0:
-            return hold_meta
-        if index == 4:
-            return hold_half
-        return hold.at[{1: 0, 2: 1, 3: 2, 5: 3, 6: 4}[index]]
-
-    greet(n, me)
-    copies = []
-    for step in range(1, n):
-        to = lax.rem(me + step, n)
-        for i, (src, dst) in enumerate(pieces(to)):
-            copy = pltpu.make_async_remote_copy(
-                src_ref=src, dst_ref=dst, send_sem=send.at[step - 1, i], recv_sem=recv.at[step - 1, i],
-                device_id={"seq": to}, device_id_type=pl.DeviceIdType.MESH,
-            )
+    def out_copies(i, far):
+        return [
+            remote(src, dst, send.at[i, far, p], recv.at[i, cross, p], 2 * layer(i) + c, 2 * y + flip(far, c))
+            for p, (src, dst) in enumerate(pieces(i, far))
+        ]
+
+    def from_row(i, side):
+        return 2 * layer(i) + flip(side, x)
+
+    def forward(i, side, keys):
+        piece = (ks if keys else vs).at[rows(from_row(i, side) * tok, tok)]
+        return remote(piece, piece, fsem_s.at[i, side], fsem_r.at[i, side], me, other)
+
+    greet([(2 * layer(i) + flip(side, x), 2 * y + core) for i in range(4) for side in range(2) for core in range(2)
+           if i or side] + [(me, other)])()
+    for i in (2, 3, 1):
+        for far in range(2):
+            for copy in out_copies(i, far):
+                copy.start()
+    for copy in out_copies(0, 1):
+        copy.start()
+
+    @pl.when(x != c)
+    def _():
+        for copy in out_copies(0, 0):
             copy.start()
-            copies.append(copy)
-    mine = pieces(me)
-    ins = [pltpu.make_async_copy(src, bounce(i), here.at[0, i]) for i, (src, _) in enumerate(mine)]
-    outs = [pltpu.make_async_copy(bounce(i), dst, here.at[1, i]) for i, (_, dst) in enumerate(mine)]
-    for c in ins:
-        c.start()
-    for c, d in zip(ins, outs):
-        c.wait()
-        d.start()
-    for d in outs:
-        d.wait()
-    for c in copies:
-        c.wait()
+
+    @pl.when(x == c)
+    def _():
+        mine = pieces(0, 0)
+        via = [hold.at[0], hold.at[1], hold.at[2], hold_half, hold.at[3], hold_meta]
+        ins = [pltpu.make_async_copy(src, mid, here.at[0, p]) for p, ((src, _), mid) in enumerate(zip(mine, via))]
+        outs = [pltpu.make_async_copy(mid, dst, here.at[1, p]) for p, ((_, dst), mid) in enumerate(zip(mine, via))]
+        for one in ins:
+            one.start()
+        for one, two in zip(ins, outs):
+            one.wait()
+            two.start()
+        for two in outs:
+            two.wait()
+
+    def arrive(i, side):
+        for p, (_, dst) in enumerate(pieces(i, 0)):
+            remote(dst, dst, send.at[i, 0, p], recv.at[i, side, p], me, other).wait_recv()
+
+    for i in (0, 1, 2, 3):
+        for side in range(2):
+            if i or side:
+                arrive(i, side)
+            else:
+                @pl.when(x != c)
+                def _():
+                    arrive(0, 0)
+
+            for keys in (True, False):
+                @pl.when((x == c) == keys)
+                def _():
+                    forward(i, side, keys).start()
+
+    for i in range(4):
+        for side in range(2):
+            for keys in (True, False):
+                @pl.when((x == c) == keys)
+                def _():
+                    forward(i, side, keys).wait_send()
+                    forward(i, side, not keys).wait_recv()
+
+        for far in range(2):
+            if i or far:
+                for copy in out_copies(i, far):
+                    copy.wait_send()
+            else:
+                @pl.when(x != c)
+                def _():
+                    for copy in out_copies(0, 0):
+                        copy.wait_send()
 
 
 def project_kernel(
@@ -159,48 +227,44 @@
     core_peer = 2 * y + 1 - c
     y_peer = 2 * (1 - y) + c
 
-    def flip(bit, value):
-        return 1 - value if bit else value
-
     def at(k):
         return 4 * flip(k & 4, mine) + 2 * flip(k & 2, zl) + flip(k & 1, x)
 
-    def remote(src, dst, send, recv, seq, hd):
-        return pltpu.make_async_remote_copy(
-            src_ref=src, dst_ref=dst, send_sem=send, recv_sem=recv,
-            device_id={"seq": seq, "head": hd}, device_id_type=pl.DeviceIdType.MESH,
-        )
-
-    barrier = pltpu.get_barrier_semaphore()
-    friends = [(at(k), head) for k in range(1, n)]
-    friends += [(at(k), core_peer) for k in range(4)] + [(me, y_peer)]
-    for seq, hd in friends:
-        pl.semaphore_signal(barrier, inc=1, device_id={"seq": seq, "head": hd}, device_id_type=pl.DeviceIdType.MESH)
+    met = greet([(at(k), 2 * y + core) for k in range(1, n) for core in range(2)] + [(me, core_peer), (me, y_peer)])
     own_w = pltpu.make_async_copy(w, wown, here.at[2])
     own_w.start()
     got_w = pltpu.make_async_copy(wgot, wpart.at[:, pl.ds(0, early)], here.at[3])
     got_w.start()
-    pl.semaphore_wait(barrier, len(friends))
-
-    pair, odd = me // 2, lax.rem(me, 2)
-    own, shared = cols(3 * pair + 2 * odd), cols(3 * pair + 1)
+    met()
+
+    own, shared = cols(3 * (me // 2) + 2 * c), cols(3 * (me // 2) + 1)
 
     def pieces(to):
         return [
             (of.at[rows(to * tok, tok)], attn.at[0, :, own]),
-            (os.at[rows(to * half, half)], attn.at[0, rows(odd * half, half), shared]),
+            (os.at[rows(to * half, half)], attn.at[0, rows(c * half, half), shared]),
         ]
 
-    back = [
-        [remote(src, dst, send1.at[k, i], recv1.at[k, i], at(k), head) for i, (src, dst) in enumerate(pieces(at(k)))]
-        for k in range(1, n)
-    ]
-    for copies in back:
-        for copy in copies:
+    def back(k):
+        return [
+            remote(src, dst, send1.at[k, p], recv1.at[k // 2, c, p], at(k), 2 * y + x)
+            for p, (src, dst) in enumerate(pieces(at(k)))
+        ]
+
+    local = [pltpu.make_async_copy(src, dst, here.at[p]) for p, (src, dst) in enumerate(pieces(me))]
+    for k in range(1, n):
+        for copy in back(k):
             copy.start()
-    local = [pltpu.make_async_copy(src, dst, here.at[i]) for i, (src, dst) in enumerate(pieces(me))]
-    for copy in local:
-        copy.start()
+
+    @pl.when(c != x)
+    def _():
+        for copy in back(0):
+            copy.start()
+
+    @pl.when(c == x)
+    def _():
+        for copy in local:
+            copy.start()
 
     def chunk(at_pair):
         return pl.ds(pl.multiple_of(3 * HD * at_pair, HD), 3 * HD)
@@ -217,13 +281,22 @@
     steps = [moves(i) for i in range(4)]
 
     def share(i):
+        for core in range(2):
+            for p, (_, dst) in enumerate(pieces(me)):
+                arrived = remote(dst, dst, send1.at[0, p], recv1.at[i, core, p], me, core_peer)
+                if i:
+                    arrived.wait_recv()
+                else:
+                    @pl.when((c != x) | (core != c))
+                    def _():
+                        arrived.wait_recv()
+
         if i == 0:
-            for copy in local:
-                copy.wait()
-        for k in (2 * i, 2 * i + 1):
-            if k:
-                for copy in back[k - 1]:
-                    copy.wait_recv()
+            @pl.when(c == x)
+            def _():
+                for copy in local:
+                    copy.wait()
+
         steps[i][1].start()
         steps[i][0].start()
 
@@ -366,9 +439,15 @@
     for unit in units[-4:]:
         finish(*unit)
 
-    for copies in back:
-        for copy in copies:
+    for k in range(1, n):
+        for copy in back(k):
             copy.wait_send()
+
+    @pl.when(c != x)
+    def _():
+        for copy in back(0):
+            copy.wait_send()
+
     for copies in steps:
         for copy in copies:
             copy.wait_send()
@@ -477,12 +556,14 @@
         in_specs=[anyspace] * 4,
         out_specs=[anyspace] * 7,
         scratch_shapes=[
-            pltpu.VMEM((5, tok, HD), queries.dtype),
+            pltpu.VMEM((4, tok, HD), queries.dtype),
             pltpu.VMEM((tok // 2, HD), queries.dtype),
             pltpu.VMEM((8, HD), jnp.int32),
-            pltpu.SemaphoreType.DMA((n - 1, 7)),
-            pltpu.SemaphoreType.DMA((n - 1, 7)),
-            pltpu.SemaphoreType.DMA((2, 7)),
+            pltpu.SemaphoreType.DMA((4, 2, 6)),
+            pltpu.SemaphoreType.DMA((4, 2, 6)),
+            pltpu.SemaphoreType.DMA((2, 6)),
+            pltpu.SemaphoreType.DMA((4, 2)),
+            pltpu.SemaphoreType.DMA((4, 2)),
         ],
         compiler_params=pltpu.CompilerParams(collective_id=0, has_side_effects=True),
         cost_estimate=pl.CostEstimate(flops=0, bytes_accessed=300_000_000, transcendentals=0),
@@ -497,7 +578,7 @@
     ids = jnp.arange(count_blocks, dtype=jnp.int32)
     hit = allowed[:, None, :] & (place[:, None, :] == ids[None, :, None] + 1)
     order = jnp.sum(jnp.where(hit, ids[None, None, :], 0), axis=2)
-    odd = lax.rem(lax.axis_index("seq"), 2).reshape(1).astype(jnp.int32)
+    odd = lax.rem(lax.axis_index("head"), 2).reshape(1).astype(jnp.int32)
 
     smem = pl.BlockSpec(memory_space=pltpu.SMEM)
     whole = pl.BlockSpec((tokens, HD), lambda j: (0, 0))
@@ -537,7 +618,7 @@
             pltpu.VMEM((4, tok // 2, wide), queries.dtype),
             pltpu.VMEM((4, tok // 2, wide), queries.dtype),
             pltpu.VMEM((4, tok // 2, wide), queries.dtype),
-            dma((n, 2)), dma((n, 2)), dma((4,)), dma((3, 4)), dma((3, 4)), dma((count,)), dma((count,)),
+            dma((n, 2)), dma((4, 2, 2)), dma((4,)), dma((3, 4)), dma((3, 4)), dma((count,)), dma((count,)),
             dma((count, 4)), dma((count, 4)), dma((count, 4)), dma((count, 4)),
             dma((count, 4)), dma((4, count)), dma((count,)),
         ],

time: 325 us -> 305 us (0.938)
  Pallas kernels: 315 us -> 292 us
    pallas_call x1, Pallas kernels: 129 us -> 110 us  [body_spread(): pl.pallas_call(functools.partial(spread_kernel, n, tok), out_shape=[big,...]
  transfers between devices with their start and end apart: 1 -> 1, of which waited for: 1 -> 1; matrix products, arithmetic and copies ran while one was open for 1% -> 1% of each run, Pallas kernels for 14% -> 15%
where the time goes in v3:
time: 305 us
  Pallas kernels  292 us (96%)
  local copies, waits for them, and re-layouts  8 us (3%)
  waiting for transfers between devices  3.62 us (1%)
    pallas_call x1, Pallas kernels, body_spread(): pl.pallas_call(functools.partial(project_kernel, n, tok, groups), out_sha...  138 us
    pallas_call x1, Pallas kernels, body_spread(): pl.pallas_call(functools.partial(spread_kernel, n, tok), out_shape=[big,...  110 us
    pallas_call x1, Pallas kernels, body_spread(): pl.pallas_call(attend_kernel, grid=(tokens // (2 * BLK),), out_shape=[big...  44.6 us
  transfers between devices with their start and end apart: 1, of which 1 were waited for; matrix products, arithmetic and copies ran while one was open for 1% of the time, Pallas kernels for 15%

profile of v3, /device:TPU:12, one launch (start us, length us, event | category | flops | bytes accessed | tf_op | source)
XLA Modules:
  0.0 304.8 jit_solution(2818147443560453960)
XLA Ops:
  0.0 0.0 copy-start
  0.0 0.8 copy.13
  0.8 1.4 slice.19
  2.1 0.0 copy-done
  2.2 0.1 pad_add_fusion
  2.2 0.6 pad.4.meta
  2.8 109.5 %spread.1 = (bf16[4096,128]{1,0:T(8,128)(2,1)}, bf16[2048,128]{1,0:T(8,128)(2,1)}, bf16[4096,128]{1,0:T(8,128)(2,1)}, bf16[4096,128]{1,0:T(8,128)(2,1)}, bf16[40...) custom-call(bf16[512,1536]{1,0:T(8,128)(2,1)} %q.1, bf16[512,1536]{1,0:T(8,128)(2,1)} %k.1, ...), custom_call_target="tpu_custom_call" | custom-call | bytes 300000000 | tf_op jit(solution)/shard_map/spread/pallas_call | solution.py:553
  112.3 0.1 collective-permute-start
  112.4 0.8 slice.20
  113.2 0.1 slice_reduce_fusion.1
  113.3 0.1 fusion.2
  113.4 0.2 reduce_window_sum.11
  113.6 0.7 slice_reduce_fusion.count_ref
  114.3 1.0 select_reduce_fusion.list_ref
  115.3 44.6 %attend.1 = (bf16[4096,128]{1,0:T(8,128)(2,1)}, bf16[2048,128]{1,0:T(8,128)(2,1)}) custom-call(s32[1]{0:T(128)} %bitcast.odd_ref, s32[16]{0:T(128)} %slice_reduce_fusion.count_ref, s32[16,16]{1,0:T(8,128)} %select_reduce_fusion.list_ref, bf16[4096,128]{1,0:T(8,128)(2,1)} %get-tuple-element.16.qf, bf16[2048,128]{1,0:T(8,128)(2,1)} %get-tuple-element.17.qs, ...), custom_call_target="tpu_custom_call" | custom-call | flops 20000000000 | bytes 8000000 | tf_op jit(solution)/shard_map/attend/pallas_call | solution.py:587
  159.9 3.6 %collective-permute-done.wgot = bf16[1536,384]{1,0:T(8,128)(2,1)S(1)} collective-permute-done((bf16[1536,384]{1,0:T(8,128)(2,1)S(1)}, bf16[1536,384]{1,0:T(8,128)(2,1)S(1)}, u32[]{:S(2)}, u32[]{:S(2)}) %collective-permute-start) | collective-permute-done | bytes 1179680 | tf_op jit(solution)/shard_map/ppermute | solution.py:601
  163.5 0.0 copy-start.1
  163.5 1.0 copy-done.1
  164.5 137.6 %project.1 = bf16[512,1536]{1,0:T(8,128)(2,1)} custom-call(bf16[4096,128]{1,0:T(8,128)(2,1)} %get-tuple-element.22.of, bf16[2048,128]{1,0:T(8,128)(2,1)} %get-tuple-element.23.os, bf16[1536,768]{1,0:T(8,128)(2,1)} %w.1, bf16[1536,384]{1,0:T(8,128)(2,1)} %copy-done.1), custom_call_target="tpu_custom_call" | custom-call | flops 10000000000 | bytes 30000000 | tf_op jit(solution)/shard_map/project/pallas_call | solution.py:606
  302.2 2.7 copy.15
  (1 shorter events, 0.0 us)
Async XLA Ops:
  0.0 2.2 copy-start
  112.3 51.2 %collective-permute-start = (bf16[1536,384]{1,0:T(8,128)(2,1)S(1)}, bf16[1536,384]{1,0:T(8,128)(2,1)S(1)}, u32[]{:S(2)}, u32[]{:S(2)}) collective-permute-start(bf16[1536,384]{1,0:T(8,128)(2,1)S(1)} %slice.19), channel_id=1, source_target_pairs={{0,16},{4,20},{8,24},{12,28},{16,0},{20,4},{24,8},{28,12},{1,17},{... | collective-permute-start | bytes 3538952 | tf_op jit(solution)/shard_map/ppermute | solution.py:601
  163.5 1.0 copy-start.1

commit v4 on v3

--- a/solution.py
+++ b/solution.py
@@ -424,19 +424,19 @@
         shard(r)
         for g in ready:
             finish(g, r - 1)
-    for g in ready:
-        finish(g, 3)
     units = [(g, r) for g in late for r in range(4)]
+    pending = [(g, 3) for g in ready]
     for i, (g, r) in enumerate(units):
         if r == 0:
             w_late(g).wait_recv()
         multiply(g, r)
-        if i >= 1:
+        if i:
             add_core(*units[i - 1])
-        if i >= 4:
-            finish(*units[i - 4])
+            pending.append(units[i - 1])
+        if i >= 3:
+            finish(*pending.pop(0))
     add_core(*units[-1])
-    for unit in units[-4:]:
+    for unit in pending + units[-1:]:
         finish(*unit)
 
     for k in range(1, n):
@@ -600,7 +600,7 @@
     w_early, _ = lax.optimization_barrier((w_out[:, :early], kf))
     w_got = lax.ppermute(w_early, "seq", [(i, (i + n // 2) % n) for i in range(n)])
     groups = [(0, 0, early), (0, early, wide - early), (1, 0, early)]
-    groups += [(1, first, HD) for first in range(early, wide, HD)]
+    groups += [(1, early, wide - early - HD), (1, wide - HD, HD)]
     count = len(groups)
     dma = pltpu.SemaphoreType.DMA
     return pl.pallas_call(

time: 305 us -> 297 us (0.974)
  Pallas kernels: 292 us -> 283 us
    pallas_call x1, Pallas kernels: 138 us -> 130 us  [body_spread(): pl.pallas_call(functools.partial(project_kernel, n, tok, groups), out_sha...]
where the time goes in v4:
time: 297 us
  Pallas kernels  283 us (95%)
  local copies, waits for them, and re-layouts  8 us (3%)
  waiting for transfers between devices  4.31 us (1%)
    pallas_call x1, Pallas kernels, body_spread(): pl.pallas_call(functools.partial(project_kernel, n, tok, groups), out_sha...  130 us
    pallas_call x1, Pallas kernels, body_spread(): pl.pallas_call(functools.partial(spread_kernel, n, tok), out_shape=[big,...  110 us
    pallas_call x1, Pallas kernels, body_spread(): pl.pallas_call(attend_kernel, grid=(tokens // (2 * BLK),), out_shape=[big...  43.9 us
  transfers between devices with their start and end apart: 1, of which 1 were waited for; matrix products, arithmetic and copies ran while one was open for 1% of the time, Pallas kernels for 15%

profile of v4, /device:TPU:12, one launch (start us, length us, event | category | flops | bytes accessed | tf_op | source)
XLA Modules:
  0.0 296.9 jit_solution(10680270789737826416)
XLA Ops:
  0.0 0.0 copy-start
  0.0 0.8 copy.13
  0.8 1.4 slice.19
  2.1 0.0 copy-done
  2.2 0.1 pad_add_fusion
  2.2 0.6 pad.4.meta
  2.8 109.5 %spread.1 = (bf16[4096,128]{1,0:T(8,128)(2,1)}, bf16[2048,128]{1,0:T(8,128)(2,1)}, bf16[4096,128]{1,0:T(8,128)(2,1)}, bf16[4096,128]{1,0:T(8,128)(2,1)}, bf16[40...) custom-call(bf16[512,1536]{1,0:T(8,128)(2,1)} %q.1, bf16[512,1536]{1,0:T(8,128)(2,1)} %k.1, ...), custom_call_target="tpu_custom_call" | custom-call | bytes 300000000 | tf_op jit(solution)/shard_map/spread/pallas_call | solution.py:553
  112.3 0.1 collective-permute-start
  112.4 0.8 slice.20
  113.2 0.1 slice_reduce_fusion.1
  113.3 0.1 fusion.2
  113.4 0.2 reduce_window_sum.11
  113.6 0.7 slice_reduce_fusion.count_ref
  114.3 1.0 select_reduce_fusion.list_ref
  115.3 43.9 %attend.1 = (bf16[4096,128]{1,0:T(8,128)(2,1)}, bf16[2048,128]{1,0:T(8,128)(2,1)}) custom-call(s32[1]{0:T(128)} %bitcast.odd_ref, s32[16]{0:T(128)} %slice_reduce_fusion.count_ref, s32[16,16]{1,0:T(8,128)} %select_reduce_fusion.list_ref, bf16[4096,128]{1,0:T(8,128)(2,1)} %get-tuple-element.16.qf, bf16[2048,128]{1,0:T(8,128)(2,1)} %get-tuple-element.17.qs, ...), custom_call_target="tpu_custom_call" | custom-call | flops 20000000000 | bytes 8000000 | tf_op jit(solution)/shard_map/attend/pallas_call | solution.py:587
  159.2 4.3 %collective-permute-done.wgot = bf16[1536,384]{1,0:T(8,128)(2,1)S(1)} collective-permute-done((bf16[1536,384]{1,0:T(8,128)(2,1)S(1)}, bf16[1536,384]{1,0:T(8,128)(2,1)S(1)}, u32[]{:S(2)}, u32[]{:S(2)}) %collective-permute-start) | collective-permute-done | bytes 1179680 | tf_op jit(solution)/shard_map/ppermute | solution.py:601
  163.5 0.0 copy-start.1
  163.5 1.0 copy-done.1
  164.5 129.7 %project.1 = bf16[512,1536]{1,0:T(8,128)(2,1)} custom-call(bf16[4096,128]{1,0:T(8,128)(2,1)} %get-tuple-element.22.of, bf16[2048,128]{1,0:T(8,128)(2,1)} %get-tuple-element.23.os, bf16[1536,768]{1,0:T(8,128)(2,1)} %w.1, bf16[1536,384]{1,0:T(8,128)(2,1)} %copy-done.1), custom_call_target="tpu_custom_call" | custom-call | flops 10000000000 | bytes 30000000 | tf_op jit(solution)/shard_map/project/pallas_call | solution.py:606
  294.2 2.7 copy.15
  (1 shorter events, 0.0 us)
Async XLA Ops:
  0.0 2.2 copy-start
  112.3 51.2 %collective-permute-start = (bf16[1536,384]{1,0:T(8,128)(2,1)S(1)}, bf16[1536,384]{1,0:T(8,128)(2,1)S(1)}, u32[]{:S(2)}, u32[]{:S(2)}) collective-permute-start(bf16[1536,384]{1,0:T(8,128)(2,1)S(1)} %slice.19), channel_id=1, source_target_pairs={{0,16},{4,20},{8,24},{12,28},{16,0},{20,4},{24,8},{28,12},{1,17},{... | collective-permute-start | bytes 3538952 | tf_op jit(solution)/shard_map/ppermute | solution.py:601
  163.5 1.0 copy-start.1

commit v5 on v4

--- a/solution.py
+++ b/solution.py
@@ -110,8 +110,8 @@
 
 
 def spread_kernel(
-    n, tok, q, k, v, meta, qf, qs, kf, ks, vf, vs, metas,
-    hold, hold_half, hold_meta, send, recv, here, fsem_s, fsem_r,
+    n, tok, q, k, v, meta, w, qf, qs, kf, ks, vf, vs, metas, w_early,
+    hold, hold_half, hold_meta, hold_w, here_w, send, recv, here, fsem_s, fsem_r,
 ):
     me, head = lax.axis_index("seq"), lax.axis_index("head")
     half = tok // 2
@@ -151,6 +151,9 @@
 
     greet([(2 * layer(i) + flip(side, x), 2 * y + core) for i in range(4) for side in range(2) for core in range(2)
            if i or side] + [(me, other)])()
+    w_in = pltpu.make_async_copy(w.at[:, pl.ds(0, w_early.shape[1])], hold_w, here_w.at[0])
+    w_out = pltpu.make_async_copy(hold_w, w_early, here_w.at[1])
+    w_in.start()
     for i in (2, 3, 1):
         for far in range(2):
             for copy in out_copies(i, far):
@@ -176,6 +179,10 @@
             two.start()
         for two in outs:
             two.wait()
+
+    w_in.wait()
+    w_out.start()
+    w_out.wait()
 
     def arrive(i, side):
         for p, (_, dst) in enumerate(pieces(i, 0)):
@@ -550,15 +557,20 @@
     anyspace = pl.BlockSpec(memory_space=pl.ANY)
     big = jax.ShapeDtypeStruct((tokens, HD), queries.dtype)
     small = jax.ShapeDtypeStruct((tokens // 2, HD), queries.dtype)
-    qf, qs, kf, ks, vf, vs, metas = pl.pallas_call(
+    deep, wide = w_out.shape
+    early = wide // 2
+    qf, qs, kf, ks, vf, vs, metas, w_early = pl.pallas_call(
         functools.partial(spread_kernel, n, tok),
-        out_shape=[big, small, big, big, big, big, jax.ShapeDtypeStruct((8 * n, HD), jnp.int32)],
-        in_specs=[anyspace] * 4,
-        out_specs=[anyspace] * 7,
+        out_shape=[big, small, big, big, big, big, jax.ShapeDtypeStruct((8 * n, HD), jnp.int32),
+                   jax.ShapeDtypeStruct((deep, early), w_out.dtype)],
+        in_specs=[anyspace] * 5,
+        out_specs=[anyspace] * 8,
         scratch_shapes=[
             pltpu.VMEM((4, tok, HD), queries.dtype),
             pltpu.VMEM((tok // 2, HD), queries.dtype),
             pltpu.VMEM((8, HD), jnp.int32),
+            pltpu.VMEM((deep, early), w_out.dtype),
+            pltpu.SemaphoreType.DMA((2,)),
             pltpu.SemaphoreType.DMA((4, 2, 6)),
             pltpu.SemaphoreType.DMA((4, 2, 6)),
             pltpu.SemaphoreType.DMA((2, 6)),
@@ -568,7 +580,7 @@
         compiler_params=pltpu.CompilerParams(collective_id=0, has_side_effects=True),
         cost_estimate=pl.CostEstimate(flops=0, bytes_accessed=300_000_000, transcendentals=0),
         name="spread",
-    )(queries, keys, values, meta)
+    )(queries, keys, values, meta, w_out)
 
     metas = metas.reshape(n, 8, HD)[:, :per].reshape(n * per, HD)
     frame, links = metas[:, 0], metas[:, 1:1 + count_blocks]
@@ -595,9 +607,6 @@
         name="attend",
     )(odd, count, order, qf, qs, kf, ks, vf, vs)
 
-    deep, wide = w_out.shape
-    early = wide // 2
-    w_early, _ = lax.optimization_barrier((w_out[:, :early], kf))
     w_got = lax.ppermute(w_early, "seq", [(i, (i + n // 2) % n) for i in range(n)])
     groups = [(0, 0, early), (0, early, wide - early), (1, 0, early)]
     groups += [(1, early, wide - early - HD), (1, wide - HD, HD)]

time: 297 us -> 296 us (level)
  no operation moved by 1% of the time
where the time goes in v5:
time: 296 us
  Pallas kernels  283 us (96%)
  local copies, waits for them, and re-layouts  6.62 us (2%)
  waiting for transfers between devices  4.3 us (1%)
    pallas_call x1, Pallas kernels, body_spread(): pl.pallas_call(functools.partial(project_kernel, n, tok, groups), out_sha...  129 us
    pallas_call x1, Pallas kernels, body_spread(): pl.pallas_call(functools.partial(spread_kernel, n, tok), out_shape=[big,...  110 us
    pallas_call x1, Pallas kernels, body_spread(): pl.pallas_call(attend_kernel, grid=(tokens // (2 * BLK),), out_shape=[big...  44.2 us
  transfers between devices with their start and end apart: 1, of which 1 were waited for; matrix products, arithmetic and copies ran while one was open for 1% of the time, Pallas kernels for 15%

profile of v5, /device:TPU:12, one launch (start us, length us, event | category | flops | bytes accessed | tf_op | source)
XLA Modules:
  0.0 296.0 jit_solution(10458915350049497606)
XLA Ops:
  0.0 0.7 copy.13
  0.7 0.8 pad_add_fusion
  1.5 0.6 pad.4.meta
  2.1 109.5 %spread.1 = (bf16[4096,128]{1,0:T(8,128)(2,1)}, bf16[2048,128]{1,0:T(8,128)(2,1)}, bf16[4096,128]{1,0:T(8,128)(2,1)}, bf16[4096,128]{1,0:T(8,128)(2,1)}, bf16[40...) custom-call(bf16[512,1536]{1,0:T(8,128)(2,1)} %q.1, ...), custom_call_target="tpu_custom_call" | custom-call | bytes 300000000 | tf_op jit(solution)/shard_map/spread/pallas_call | solution.py:562
  111.6 0.1 collective-permute-start
  111.7 0.8 slice.16
  112.5 0.1 slice_reduce_fusion.1
  112.6 0.1 fusion.2
  112.7 0.2 reduce_window_sum.11
  112.8 0.7 slice_reduce_fusion.count_ref
  113.6 1.0 select_reduce_fusion.list_ref
  114.6 44.2 %attend.1 = (bf16[4096,128]{1,0:T(8,128)(2,1)}, bf16[2048,128]{1,0:T(8,128)(2,1)}) custom-call(s32[1]{0:T(128)} %bitcast.odd_ref, s32[16]{0:T(128)} %slice_reduce_fusion.count_ref, s32[16,16]{1,0:T(8,128)} %select_reduce_fusion.list_ref, bf16[4096,128]{1,0:T(8,128)(2,1)} %get-tuple-element.16.qf, bf16[2048,128]{1,0:T(8,128)(2,1)} %get-tuple-element.17.qs, ...), custom_call_target="tpu_custom_call" | custom-call | flops 20000000000 | bytes 8000000 | tf_op jit(solution)/shard_map/attend/pallas_call | solution.py:599
  158.8 4.3 %collective-permute-done.wgot = bf16[1536,384]{1,0:T(8,128)(2,1)S(1)} collective-permute-done((bf16[1536,384]{1,0:T(8,128)(2,1)}, bf16[1536,384]{1,0:T(8,128)(2,1)S(1)}, u32[]{:S(2)}, u32[]{:S(2)}) %collective-permute-start) | collective-permute-done | bytes 1179680 | tf_op jit(solution)/shard_map/ppermute | solution.py:610
  163.1 0.0 copy-start
  163.1 1.0 copy-done
  164.1 129.2 %project.1 = bf16[512,1536]{1,0:T(8,128)(2,1)} custom-call(bf16[4096,128]{1,0:T(8,128)(2,1)} %get-tuple-element.22.of, bf16[2048,128]{1,0:T(8,128)(2,1)} %get-tuple-element.23.os, bf16[1536,768]{1,0:T(8,128)(2,1)} %w.3, bf16[1536,384]{1,0:T(8,128)(2,1)} %copy-done), custom_call_target="tpu_custom_call" | custom-call | flops 10000000000 | bytes 30000000 | tf_op jit(solution)/shard_map/project/pallas_call | solution.py:615
  293.4 2.7 copy.15
  (1 shorter events, 0.0 us)
Async XLA Ops:
  111.6 51.5 %collective-permute-start = (bf16[1536,384]{1,0:T(8,128)(2,1)}, bf16[1536,384]{1,0:T(8,128)(2,1)S(1)}, u32[]{:S(2)}, u32[]{:S(2)}) collective-permute-start(bf16[1536,384]{1,0:T(8,128)(2,1)} %get-tuple-element.24), channel_id=1, source_target_pairs={{0,16},{4,20},{8,24},{12,28},{16,0},{20,4},{24,8},{28,12},{1,17},{... | collective-permute-start | bytes 3538952 | tf_op jit(solution)/shard_map/ppermute | solution.py:610
  163.1 1.0 copy-start

commit v6 on v5

--- a/solution.py
+++ b/solution.py
@@ -429,10 +429,11 @@
         for i in range(4):
             steps[i][(None, 0, 1, 2)[r]].wait_recv() if r != 2 else None
         shard(r)
-        for g in ready:
-            finish(g, r - 1)
+        if r > 1:
+            for g in ready:
+                finish(g, r - 2)
     units = [(g, r) for g in late for r in range(4)]
-    pending = [(g, 3) for g in ready]
+    pending = [(g, r) for r in (2, 3) for g in ready]
     for i, (g, r) in enumerate(units):
         if r == 0:
             w_late(g).wait_recv()
@@ -440,7 +441,9 @@
         if i:
             add_core(*units[i - 1])
             pending.append(units[i - 1])
-        if i >= 3:
+        if i >= 1:
+            finish(*pending.pop(0))
+        if i in (2, 4, 6):
             finish(*pending.pop(0))
     add_core(*units[-1])
     for unit in pending + units[-1:]:

time: 296 us -> 293 us (0.990)
  Pallas kernels: 283 us -> 280 us
    pallas_call x1, Pallas kernels: 129 us -> 125 us  [body_spread(): pl.pallas_call(functools.partial(project_kernel, n, tok, groups), out_sha...]
  transfers between devices with their start and end apart: 1 -> 1, of which waited for: 1 -> 1; matrix products, arithmetic and copies ran while one was open for 1% -> 1% of each run, Pallas kernels for 15% -> 16%
where the time goes in v6:
time: 293 us; the launch traced here: 292 us
  Pallas kernels  280 us (96%)
  local copies, waits for them, and re-layouts  6.62 us (2%)
  waiting for transfers between devices  3.23 us (1%)
    pallas_call x1, Pallas kernels, body_spread(): pl.pallas_call(functools.partial(project_kernel, n, tok, groups), out_sha...  125 us
    pallas_call x1, Pallas kernels, body_spread(): pl.pallas_call(functools.partial(spread_kernel, n, tok), out_shape=[big,...  110 us
    pallas_call x1, Pallas kernels, body_spread(): pl.pallas_call(attend_kernel, grid=(tokens // (2 * BLK),), out_shape=[big...  45.3 us
  transfers between devices with their start and end apart: 1, of which 1 were waited for; matrix products, arithmetic and copies ran while one was open for 1% of the time, Pallas kernels for 16%

profile of v6, /device:TPU:12, one launch (start us, length us, event | category | flops | bytes accessed | tf_op | source)
XLA Modules:
  0.0 292.1 jit_solution(9499295891732553021)
XLA Ops:
  0.0 0.7 copy.13
  0.7 0.8 pad_add_fusion
  1.5 0.6 pad.4.meta
  2.1 109.5 %spread.1 = (bf16[4096,128]{1,0:T(8,128)(2,1)}, bf16[2048,128]{1,0:T(8,128)(2,1)}, bf16[4096,128]{1,0:T(8,128)(2,1)}, bf16[4096,128]{1,0:T(8,128)(2,1)}, bf16[40...) custom-call(bf16[512,1536]{1,0:T(8,128)(2,1)} %q.1, ...), custom_call_target="tpu_custom_call" | custom-call | bytes 300000000 | tf_op jit(solution)/shard_map/spread/pallas_call | solution.py:565
  111.6 0.1 collective-permute-start
  111.7 0.8 slice.16
  112.5 0.1 slice_reduce_fusion.1
  112.6 0.1 fusion.2
  112.7 0.2 reduce_window_sum.11
  112.8 0.7 slice_reduce_fusion.count_ref
  113.6 1.0 select_reduce_fusion.list_ref
  114.6 45.3 %attend.1 = (bf16[4096,128]{1,0:T(8,128)(2,1)}, bf16[2048,128]{1,0:T(8,128)(2,1)}) custom-call(s32[1]{0:T(128)} %bitcast.odd_ref, s32[16]{0:T(128)} %slice_reduce_fusion.count_ref, s32[16,16]{1,0:T(8,128)} %select_reduce_fusion.list_ref, bf16[4096,128]{1,0:T(8,128)(2,1)} %get-tuple-element.16.qf, bf16[2048,128]{1,0:T(8,128)(2,1)} %get-tuple-element.17.qs, ...), custom_call_target="tpu_custom_call" | custom-call | flops 20000000000 | bytes 8000000 | tf_op jit(solution)/shard_map/attend/pallas_call | solution.py:602
  159.9 3.2 %collective-permute-done.wgot = bf16[1536,384]{1,0:T(8,128)(2,1)S(1)} collective-permute-done((bf16[1536,384]{1,0:T(8,128)(2,1)}, bf16[1536,384]{1,0:T(8,128)(2,1)S(1)}, u32[]{:S(2)}, u32[]{:S(2)}) %collective-permute-start) | collective-permute-done | bytes 1179680 | tf_op jit(solution)/shard_map/ppermute | solution.py:613
  163.1 0.0 copy-start
  163.1 1.0 copy-done
  164.1 125.3 %project.1 = bf16[512,1536]{1,0:T(8,128)(2,1)} custom-call(bf16[4096,128]{1,0:T(8,128)(2,1)} %get-tuple-element.22.of, bf16[2048,128]{1,0:T(8,128)(2,1)} %get-tuple-element.23.os, bf16[1536,768]{1,0:T(8,128)(2,1)} %w.3, bf16[1536,384]{1,0:T(8,128)(2,1)} %copy-done), custom_call_target="tpu_custom_call" | custom-call | flops 10000000000 | bytes 30000000 | tf_op jit(solution)/shard_map/project/pallas_call | solution.py:618
  289.4 2.7 copy.15
  (1 shorter events, 0.0 us)
Async XLA Ops:
  111.6 51.5 %collective-permute-start = (bf16[1536,384]{1,0:T(8,128)(2,1)}, bf16[1536,384]{1,0:T(8,128)(2,1)S(1)}, u32[]{:S(2)}, u32[]{:S(2)}) collective-permute-start(bf16[1536,384]{1,0:T(8,128)(2,1)} %get-tuple-element.24), channel_id=1, source_target_pairs={{0,16},{4,20},{8,24},{12,28},{16,0},{20,4},{24,8},{28,12},{1,17},{... | collective-permute-start | bytes 3538952 | tf_op jit(solution)/shard_map/ppermute | solution.py:613
  163.1 1.0 copy-start
